TPU v7x, 512 devices: a whole 4x4x16 slice. The times are simulated.
512 devices in a mesh: seq: 16 (over y, z_hi), mp: 32 (over z_lo, x, core).
Axes of the slice: x: 4, y: 4, z: 16 (z_hi: 4, z_lo: 4; z = z_hi * 4 + z_lo), core: 2. Of those that a mesh axis runs over, the one named last changes fastest.
Arguments:
- incoming: bfloat16 [8192, 4096], P('seq', 'mp'), may hold values from -12 to 12
- queries: bfloat16 [8192, 4096], P('seq', 'mp'), may hold values from -5 to 5
- key_vecs: bfloat16 [8192, 4096], P('seq', 'mp'), may hold values from -5 to 5
- value_vecs: bfloat16 [8192, 4096], P('seq', 'mp'), may hold values from -6 to 6
- w_out: bfloat16 [4096, 4096], P(None, 'mp'), may hold values from -0.09375 to 0.09375
- norm_gain: float32 [4096], P('mp'), may hold values from 0.25 to 1.75
- filters: bfloat16 [4096, 256], P('mp'), may hold values from -0.375 to 0.375
- filter_len: int32 [4096], P('mp'), may hold values from 128 to 256, as said below
- skip_gain: float32 [4096], P('mp'), may hold values from 0.5 to 1.5
- slot_map: int32 [32], replicated, may hold values from 0 to 31, as said below
Outputs:
- layer_out: bfloat16 [8192, 4096], P('seq', 'mp')
Inputs may be any that keep to these rules, and one draw needn't show every extreme that they name: `slot_map`: slots 2 * i and 2 * i + 1, the rows of index i of seq, hold blocks i and 31 - i, in either order. `filter_len`: some channel uses all 256 taps.
All inputs are finite; a program needn't handle non-finite values.
Results may differ from a plain program's by a relative error of at most 0.0055.
Values may be sent and summed in bfloat16 or wider, within the bound.
A program may use at most 64 MiB of HBM per device.

v0:
```python
import math

import jax
import jax.numpy as jnp
from jax import lax
from jax.sharding import PartitionSpec as P

D = 4096
HD = 128


EPS = 1e-05
NEG = -1e30


def in_one_piece(arrays, axis, dim, along):
    widths = [a.shape[along] for a in arrays]
    both = jnp.concatenate(arrays, axis=along)
    result = lax.all_gather(both, axis, axis=dim, tiled=True)
    return tuple(jnp.split(result, [sum(widths[:k]) for k in range(1, len(widths))], axis=along))


def from_everyone(x, axis):
    size = lax.axis_size(axis)
    return lax.all_to_all(jnp.broadcast_to(x[None], (size, *x.shape)), axis, 0, 0, tiled=True)


def of_everyone(x, axis):
    everything = from_everyone(x, axis)
    return jnp.sum(everything, axis=0)


def shifted(block, axis, distance):
    devices = range(lax.axis_size(axis))
    route = [(i - distance, i) for i in devices if i - distance in devices]
    return lax.ppermute(block, axis, route)


def block_update(running, query_heads, query_pos, key_part, value_part, key_pos):
    peak_now, total_now, accum_now = running
    key_count = key_part.shape[0]
    head_count = query_heads.shape[1]
    key_heads = key_part.reshape(key_count, head_count, HD)
    value_heads = value_part.reshape(key_count, head_count, HD)
    scores = jnp.einsum(
        "thd,shd->ths", query_heads, key_heads, preferred_element_type=jnp.float32
    ) * HD ** (-0.5)
    allowed = key_pos[None, None, :] <= query_pos[:, None, None]
    masked = jnp.where(allowed, scores, NEG)
    peak_next = jnp.maximum(peak_now, jnp.max(masked, axis=2))
    weights = jnp.where(allowed, jnp.exp(masked - peak_next[:, :, None]), 0.0)
    factor = jnp.exp(peak_now - peak_next)
    total_next = total_now * factor + jnp.sum(weights, axis=2)
    summed = jnp.einsum(
        "ths,shd->thd",
        weights.astype(jnp.bfloat16),
        value_heads,
        preferred_element_type=jnp.float32,
    )
    accum_next = accum_now * factor[:, :, None] + summed
    return (peak_next, total_next, accum_next)


def guarded_update(running, query_heads, query_pos, key_part, value_part, key_pos):
    return block_update(running, query_heads, query_pos, key_part, value_part, key_pos)


def attend_keys(running, query_heads, query_pos, key_part, value_part, key_pos):
    key_count = key_part.shape[0]
    block_rows = 1024
    block_count = key_count // block_rows

    def attend_advance(state, block_item):
        return (
            guarded_update(
                state, query_heads, query_pos, block_item[0], block_item[1], block_item[2]
            ),
            None,
        )

    stacked = (
        key_part.reshape(block_count, block_rows, -1),
        value_part.reshape(block_count, block_rows, -1),
        key_pos.reshape(block_count, block_rows),
    )
    running, _ = lax.scan(attend_advance, running, stacked)
    return running


def causal_window(extended, taps_lag):
    pair_count, twice, width = extended.shape
    length = twice // 2
    tap_count = taps_lag.shape[0]
    inner = math.gcd(tap_count, 16)

    def causal_advance(block, accum):
        base = block * inner
        window = lax.dynamic_slice_in_dim(
            extended, length - base - inner + 1, length + inner - 1, 1
        ).astype(jnp.float32)
        tap_block = lax.dynamic_slice_in_dim(taps_lag, base, inner, 0).astype(jnp.float32)
        for lag in range(inner):
            offset = inner - 1 - lag
            accum = accum + tap_block[lag][None, None, :] * window[:, offset : offset + length]
        return accum

    start = jnp.zeros((pair_count, length, width), jnp.float32)
    return lax.fori_loop(0, tap_count // inner, causal_advance, start)


def on_device(
    incoming,
    queries,
    key_vecs,
    value_vecs,
    w_out,
    norm_gain,
    filters,
    filter_len,
    skip_gain,
    slot_map,
):
    tok_rows, local_width = queries.shape
    span_rows = tok_rows // 2
    head_count = local_width // HD
    all_rows = slot_map.shape[0] * span_rows
    row_ids = jnp.arange(all_rows, dtype=jnp.int32)
    position = (
        jnp.repeat(slot_map, span_rows, total_repeat_length=all_rows) * span_rows
        + row_ids % span_rows
    )
    seq_rank = lax.axis_index("seq")
    seq_size = lax.axis_size("seq")
    own_pos = lax.dynamic_slice_in_dim(position, seq_rank * tok_rows, tok_rows)
    query_heads = queries.reshape(tok_rows, head_count, HD)
    piece = in_one_piece((key_vecs, value_vecs), "seq", 0, 1)
    key_pos = lax.slice_in_dim(position, 0, piece[0].shape[0], axis=0)
    running = attend_keys(
        (
            jnp.full((tok_rows, head_count), NEG, jnp.float32),
            jnp.zeros((tok_rows, head_count), jnp.float32),
            jnp.zeros((tok_rows, head_count, HD), jnp.float32),
        ),
        query_heads,
        own_pos,
        piece[0],
        piece[1],
        key_pos,
    )
    attention = (running[2] / running[1][:, :, None]).reshape(-1, local_width).astype(jnp.bfloat16)
    projected = jnp.dot(
        lax.all_gather(attention, "mp", axis=1, tiled=True),
        w_out,
        preferred_element_type=jnp.float32,
    )
    residual = incoming.astype(jnp.float32) + projected
    square_total = of_everyone(jnp.sum(residual * residual, axis=1), "mp")
    normed = (residual * lax.rsqrt(square_total / D + EPS)[:, None] * norm_gain[None, :]).astype(
        jnp.bfloat16
    )
    tap_count = filters.shape[1]
    taps = jnp.where(
        jnp.arange(tap_count, dtype=jnp.int32)[None, :] < filter_len[:, None],
        filters,
        jnp.zeros((), filters.dtype),
    )
    taps_lag = taps.T
    pair_ids = lax.dynamic_slice_in_dim(slot_map, 2 * seq_rank, 2)
    low_first = pair_ids[0] < pair_ids[1]
    slots = normed.reshape(2, span_rows, local_width)
    low_rows = jnp.where(low_first, slots[0], slots[1])
    high_rows = jnp.where(low_first, slots[1], slots[0])
    own_pair = jnp.stack([low_rows, high_rows])
    last_rank = seq_rank == seq_size - 1
    low_before = shifted(own_pair[0], "seq", 1)
    high_before = shifted(own_pair[1], "seq", -1)
    high_before = jnp.where(last_rank, own_pair[0], high_before)
    before_pair = jnp.stack([low_before, high_before])
    conv_pair = causal_window(jnp.concatenate([before_pair, own_pair], axis=1), taps_lag)
    conv_slots = jnp.where(low_first, conv_pair, conv_pair[::-1])
    conv_rows = conv_slots.reshape(tok_rows, local_width)
    layer_out = residual + conv_rows + skip_gain[None, :] * normed.astype(jnp.float32)
    return layer_out.astype(jnp.bfloat16)


def solution(mesh):
    placed = (
        P("seq", "mp"),
        P("seq", "mp"),
        P("seq", "mp"),
        P("seq", "mp"),
        P(None, "mp"),
        P("mp"),
        P("mp", None),
        P("mp"),
        P("mp"),
        P(),
    )
    return jax.shard_map(
        on_device, mesh=mesh, in_specs=placed, out_specs=P("seq", "mp"), check_vma=False
    )
```

profile of v0, /device:TPU:1, one launch (start us, length us, event | category | flops | bytes accessed | tf_op | source)
XLA Modules:
  0.0 308.7 jit_solution(983275988163275576)
XLA Ops:
  6.5 1.8 pad_maximum_fusion
  8.4 1.8 fusion.60
  10.3 2.1 fusion.59
  12.3 21.1 %select_multiply_fusion.1 = s32[8192]{0:T(1024)S(1)} fusion(pred[8192]{0:T(1024)(128)(4,1)} %constant.283, pred[8192]{0:T(1024)(128)(4,1)} %constant.284, pred[8192]{0:T(1024)(128)(4,1)} %constant.285, pred[8192]{0:T(1024)(128)(4,1)} %constant.286, pred[8192]{0:T(1024)(128)(4,1)} %constant.287, pred[8192]{0:T(1024)(128)(4,1)} %constant.288, ...), kind=kLoop, calls=%fused_computation.106 | loop fusion | flops 262144 | bytes 286848 | tf_op jit(solution)/shard_map/mul | solution.py:129
  33.5 116.5 %all-gather.4.cloned.1.call-done = bf16[8192,256]{1,0:T(8,128)(2,1)} async-done(((bf16[512,256]{1,0:T(8,128)(2,1)}), bf16[8192,256]{1,0:T(8,128)(2,1)}) %all-gather.4.cloned.1.call-update) | async-done | bytes 4194320 | tf_op jit(solution)/shard_map/all_gather | solution.py:19
  150.0 4.5 %fusion.57 = (bf16[8192,128]{1,0:T(8,128)(2,1)}, bf16[8192,128]{1,0:T(8,128)(2,1)}) fusion(bf16[8192,256]{1,0:T(8,128)(2,1)} %all-gather.4.cloned.1.call-done), kind=kLoop, calls=%fused_computation.114 | loop fusion | bytes 8388608 | tf_op jit(solution)/shard_map/split | solution.py:20
  154.5 32.2 %while.34 = (s32[]{:T(128)}, f32[512,1]{0,1:T(1,128)S(1)}, f32[512,1]{0,1:T(1,128)S(1)}, f32[512,1,128]{0,2,1:T(8,128)S(1)}, s32[8,1024]{1,0:T(8,128)S(1)}, /*in...) while((s32[]{:T(128)}, f32[512,1]{0,1:T(1,128)S(1)}, ...), condition=%wide.region_3.4_spmd.clone, body=%wide.region_0.3_spmd.clone.sunk | while | flops 277023232 | bytes 7531645 | solution.py:86
  156.6 1.9 fusion.77
  158.5 1.4 fusion.73
  160.6 1.9 fusion.77
  164.7 1.9 fusion.77
  168.7 1.9 fusion.77
  172.7 1.9 fusion.77
  176.8 1.9 fusion.77
  178.7 1.4 fusion.73
  180.8 1.9 fusion.77
  184.8 1.9 fusion.77
  187.5 63.7 %all-gather.6.cloned.1.call-done = bf16[512,1,4096]{0,2,1:T(8,128)(2,1)} async-done(((bf16[512,1,128]{0,2,1:T(8,128)(2,1)}), bf16[512,1,4096]{0,2,1:T(8,128)(2,1)}) %all-gather.6.cloned.1.call-update) | async-done | bytes 4194320 | tf_op jit(solution)/shard_map/all_gather | solution.py:152
  251.1 3.6 %multiply_reduce_fusion = (f32[512]{0:T(512)S(1)}, f32[512,128]{1,0:T(8,128)S(1)}) fusion(bf16[4096,128]{1,0:T(8,128)(2,1)S(1)} %copy-done, bf16[512,1,4096]{0,2,1:T(8,128)(2,1)} %all-gather.6.cloned.1.call-done, bf16[512,128]{1,0:T(8,128)(2,1)} %param.16), kind=kOutput, calls=%fused_computation.93 | convolution fusion | flops 537132544 | bytes 5638144 | tf_op jit(solution)/shard_map/dot_general | solution.py:151
  255.4 5.4 %all-to-all-start = ((f32[32,1,512]{2,1,0:T(1,128)}), f32[32,1,512]{2,1,0:T(1,128)S(1)}, u32[]{:S(2)}, u32[]{:S(2)}) async-start(f32[32,1,512]{2,1,0:T(1,128)} %broadcast_in_dim.58), calls=%async_computation | async-start | bytes 131072 | tf_op jit(solution)/shard_map/all_to_all | solution.py:25
  262.8 5.7 %all-to-all-done = f32[32,1,512]{2,1,0:T(1,128)S(1)} async-done(((f32[32,1,512]{2,1,0:T(1,128)}), f32[32,1,512]{2,1,0:T(1,128)S(1)}, u32[]{:S(2)}, u32[]{:S(2)}) %all-to-all-start) | async-done | bytes 65568 | tf_op jit(solution)/shard_map/all_to_all | solution.py:25
  270.1 12.8 %collective-permute-done.1 = bf16[256,128]{1,0:T(8,128)(2,1)S(1)} collective-permute-done((bf16[256,128]{1,0:T(8,128)(2,1)S(1)}, bf16[256,128]{1,0:T(8,128)(2,1)S(1)}, u32[]{:S(2)}, u32[]{:S(2)}) %collective-permute-start.1) | collective-permute-done | bytes 65568 | tf_op jit(solution)/shard_map/ppermute | solution.py:36
  282.9 7.3 %collective-permute-start = (bf16[256,128]{1,0:T(8,128)(2,1)S(1)}, bf16[256,128]{1,0:T(8,128)(2,1)S(1)}, u32[]{:S(2)}, u32[]{:S(2)}) collective-permute-start(bf16[256,128]{1,0:T(8,128)(2,1)S(1)} %get-tuple-element.284), channel_id=1, source_target_pairs={{0,32},{32,64},{64,96},{96,128},{128,160},{160,192},{192,224},{224... | collective-permute-start | bytes 196616 | tf_op jit(solution)/shard_map/ppermute | solution.py:36
  291.6 9.5 %while.35 = (s32[]{:T(128)}, f32[2,256,128]{2,1,0:T(8,128)S(1)}, bf16[256,128]{1,0:T(8,128)(2,1)S(1)}, bf16[2,512,128]{2,1,0:T(8,128)(2,1)S(1)}, s32[]{:T(128)},...) while((s32[]{:T(128)}, f32[2,256,128]{2,1,0:T(8,128)S(1)}, ...), condition=%wide.region_7.8_spmd.clone, body=%wide.region_6.7_spmd.clone.sunk | while | flops 2234123 | bytes 5171923 | solution.py:108
  (150 shorter events, 28.6 us)
Async XLA Ops:
  6.5 244.6 %copy-start = (bf16[4096,128]{1,0:T(8,128)(2,1)S(1)}, bf16[4096,128]{1,0:T(8,128)(2,1)}, u32[]{:S(2)}) copy-start(bf16[4096,128]{1,0:T(8,128)(2,1)} %param.20) | copy-start | bytes 3145732
  6.5 143.5 %all-gather.4.cloned.1.call-start = ((), (), s32[]{:S(2)}) async-start(), calls=%async_computation.1 | async-start | bytes 4456448 | tf_op jit(solution)/shard_map/all_gather | solution.py:19
  8.3 242.8 %all-gather.6.cloned.1.call-start = ((), (), s32[]{:S(2)}) async-start(), calls=%async_computation.2 | async-start | bytes 4325376 | tf_op jit(solution)/shard_map/all_gather | solution.py:152
  187.4 73.4 %copy-start.1 = (s32[32]{0:T(128)S(1)}, s32[32]{0:T(128)}, u32[]{:S(2)}) copy-start(s32[32]{0:T(128)} %param.25) | copy-start | bytes 388
  187.4 73.5 %copy-start.2 = (bf16[128,256]{1,0:T(8,128)(2,1)S(1)}, bf16[128,256]{1,0:T(8,128)(2,1)}, u32[]{:S(2)}) copy-start(bf16[128,256]{1,0:T(8,128)(2,1)} %param.22) | copy-start | bytes 196612
  187.4 81.2 %copy-start.3 = (f32[128]{0:T(128)S(1)}, f32[128]{0:T(128)}, u32[]{:S(2)}) copy-start(f32[128]{0:T(128)} %param.21) | copy-start | bytes 1540
  187.5 82.6 %copy-start.4 = (s32[128]{0:T(128)S(1)}, s32[128]{0:T(128)}, u32[]{:S(2)}) copy-start(s32[128]{0:T(128)} %param.23) | copy-start | bytes 1540
  255.4 13.1 %all-to-all-start = ((f32[32,1,512]{2,1,0:T(1,128)}), f32[32,1,512]{2,1,0:T(1,128)S(1)}, u32[]{:S(2)}, u32[]{:S(2)}) async-start(f32[32,1,512]{2,1,0:T(1,128)} %broadcast_in_dim.58), calls=%async_computation | async-start | bytes 131072 | tf_op jit(solution)/shard_map/all_to_all | solution.py:25
  268.8 14.1 %collective-permute-start.1 = (bf16[256,128]{1,0:T(8,128)(2,1)S(1)}, bf16[256,128]{1,0:T(8,128)(2,1)S(1)}, u32[]{:S(2)}, u32[]{:S(2)}) collective-permute-start(bf16[256,128]{1,0:T(8,128)(2,1)S(1)} %broadcast_select_fusion.2), channel_id=1, source_target_pairs={{32,0},{64,32},{96,64},{128,96},{160,128},{192,160},{224,192},{256... | collective-permute-start | bytes 196616 | tf_op jit(solution)/shard_map/ppermute | solution.py:36
  282.9 8.6 %collective-permute-start = (bf16[256,128]{1,0:T(8,128)(2,1)S(1)}, bf16[256,128]{1,0:T(8,128)(2,1)S(1)}, u32[]{:S(2)}, u32[]{:S(2)}) collective-permute-start(bf16[256,128]{1,0:T(8,128)(2,1)S(1)} %get-tuple-element.284), channel_id=1, source_target_pairs={{0,32},{32,64},{64,96},{96,128},{128,160},{160,192},{192,224},{224... | collective-permute-start | bytes 196616 | tf_op jit(solution)/shard_map/ppermute | solution.py:36
  291.6 9.5 %copy-start.5 = (f32[128]{0:T(128)S(1)}, f32[128]{0:T(128)}, u32[]{:S(2)}) copy-start(f32[128]{0:T(128)} %param.24) | copy-start | bytes 1540
Sparse Core Ops, SparseCore 0:
  10.3 139.6 all-gather.3
  187.5 63.5 all-gather.5
where the time goes:
time: 313 us; the launch traced here: 309 us
  waiting for transfers between devices  200 us (64%)
  other arithmetic  38.3 us (12%)
  matrix products  30.1 us (10%)
  between operations  14.8 us (5%)
  starting transfers between devices  14 us (4%)
  local copies, waits for them, and re-layouts  10.2 us (3%)
    all_gather x1, waiting for transfers between devices, in_one_piece(): result = lax.all_gather(both, axis, axis=dim, tiled=True)  116 us
    all_gather x1, waiting for transfers between devices, on_device(): lax.all_gather(attention, 'mp', axis=1, tiled=True)  63.7 us
    mul x1, other arithmetic, on_device(): jnp.repeat(slot_map, span_rows, total_repeat_length=all_rows) * span_rows  21.1 us
    dot_general x8, matrix products, block_update(): jnp.einsum('ths,shd->thd', weights.astype(jnp.bfloat16), value_heads, pre...  14.9 us
    ppermute x2, waiting for transfers between devices, shifted(): return lax.ppermute(block, axis, route)  14.1 us
    dot_general x8, matrix products, block_update(): jnp.einsum('thd,shd->ths', query_heads, key_heads, preferred_element_type...  11.6 us
    ppermute x2, starting transfers between devices, shifted(): return lax.ppermute(block, axis, route)  8.56 us
    add x16, other arithmetic, causal_advance(): accum + tap_block[lag][None, None, :] * window[:, offset:offset + length]  7.57 us
  transfers between devices with their start and end apart: 5, of which 5 were waited for; matrix products, arithmetic and copies ran while one was open for 8% of the time, Pallas kernels for 0%

commit v1 on v0

v1 whole, which is shorter than its diff:
```python
import functools
import math

import jax
import jax.numpy as jnp
from jax import lax
from jax.experimental import pallas as pl
from jax.experimental.pallas import tpu as pltpu
from jax.sharding import PartitionSpec as P

D = 4096
HD = 128
SPAN = 256
EPS = 1e-05
NEG = -1e30
LOG2 = HD ** (-0.5) * math.log2(math.e)
BF = jnp.bfloat16
F32 = jnp.float32


def remote(src, dst, send_sem, recv_sem, seq):
    return pltpu.make_async_remote_copy(
        src_ref=src,
        dst_ref=dst,
        send_sem=send_sem,
        recv_sem=recv_sem,
        device_id={"seq": seq},
        device_id_type=pl.DeviceIdType.MESH,
    )


def greet(peers):
    barrier = pltpu.get_barrier_semaphore()
    for peer in peers:
        pl.semaphore_signal(
            barrier, inc=1, device_id=peer, device_id_type=pl.DeviceIdType.MESH
        )
    pl.semaphore_wait(barrier, len(peers))


def to_lanes(rep):
    return jnp.concatenate(
        [rep[k : k + 128].T[0:1] for k in range(0, rep.shape[0], 128)], axis=0
    )


def from_lanes(rows):
    return jnp.concatenate(
        [jnp.broadcast_to(rows[k : k + 1], (128, 128)).T for k in range(rows.shape[0])], axis=0
    )


def attention_kernel(
    slot_ref,
    q_ref,
    k_ref,
    v_ref,
    out_ref,
    qb,
    kvb,
    acc,
    peak,
    total,
    osend,
    lsend,
    orecv,
    lrecv,
    q_ssem,
    q_rsem,
    kv_ssem,
    kv_rsem,
    o_ssem,
    o_rsem,
    l_ssem,
    l_rsem,
):
    rank = lax.axis_index("seq")
    y, zh = rank // 4, rank % 4
    along_y = [((y + d) % 4) * 4 + zh for d in range(4)]
    along_z = [y * 4 + (zh + d) % 4 for d in range(4)]
    gap = slot_ref[2 * rank] - slot_ref[2 * rank + 1]
    straight = jnp.full((SPAN, HD), gap, jnp.int32) < 0

    def in_order(ref, half):
        one, two = ref[0:SPAN, :].astype(F32), ref[SPAN : 2 * SPAN, :].astype(F32)
        return jnp.where(straight, (one, two)[half], (two, one)[half]).astype(BF)

    for half in range(2):
        qb[0, half] = in_order(q_ref, half)
        kvb[0, half, 0] = in_order(k_ref, half)
        kvb[0, half, 1] = in_order(v_ref, half)
    greet([{"seq": along_y[d]} for d in (1, 2, 3)] + [{"seq": along_z[d]} for d in (1, 3)])

    def kv_copy(direction, half, sub, relay):
        source = 0 if not relay else (3 if direction == 0 else 1)
        target = 2 if relay else (3 if direction == 0 else 1)
        rows = pl.ds(sub * 128, 128)
        return remote(
            kvb.at[source, half, :, rows],
            kvb.at[target, half, :, rows],
            kv_ssem.at[direction, half, 2 if relay else sub],
            kv_rsem.at[target, half, sub],
            along_z[1 if direction == 0 else 3],
        )

    def kv_arrival(slot, half, sub):
        rows = pl.ds(sub * 128, 128)
        view = kvb.at[slot, half, :, rows]
        return remote(view, view, kv_ssem.at[0, half, sub], kv_rsem.at[slot, half, sub], rank)

    def q_copy(d):
        return remote(qb.at[0], qb.at[4 - d], q_ssem.at[d - 1], q_rsem.at[3 - d], along_y[d])

    def o_copies(d, half):
        return (
            remote(
                osend.at[d - 1, half],
                orecv.at[3 - d, half],
                o_ssem.at[d - 1, half],
                o_rsem.at[3 - d, half],
                along_y[d],
            ),
            remote(
                lsend.at[d - 1, half],
                lrecv.at[3 - d, half],
                l_ssem.at[d - 1, half],
                l_rsem.at[3 - d, half],
                along_y[d],
            ),
        )

    for sub in range(2):
        kv_copy(0, 0, sub, False).start()
        kv_copy(1, 0, 1 - sub, False).start()
    for d in (1, 3, 2):
        q_copy(d).start()

    acc[...] = jnp.zeros_like(acc)
    total[...] = jnp.zeros_like(total)
    peak[...] = jnp.full_like(peak, NEG)
    ones = jnp.ones((SPAN, HD), BF)

    def block(d, qhalf, slot, half, diagonal):
        keys, values = kvb[slot, half, 0], kvb[slot, half, 1]
        scores = lax.dot_general(
            qb[d, qhalf], keys, (((1,), (1,)), ((), ())), preferred_element_type=F32
        )
        if diagonal:
            row = lax.broadcasted_iota(jnp.int32, (SPAN, SPAN), 0)
            col = lax.broadcasted_iota(jnp.int32, (SPAN, SPAN), 1)
            scores = jnp.where(col <= row, scores, NEG)
        old = peak[d, qhalf]
        new = jnp.maximum(old, jnp.max(scores, axis=1, keepdims=True))
        weights = jnp.exp2((scores - jnp.concatenate([new, new], axis=1)) * LOG2)
        factor = jnp.exp2((old - new) * LOG2)
        summed = lax.dot_general(
            weights.astype(BF),
            jnp.concatenate([values, ones], axis=1),
            (((1,), (0,)), ((), ())),
            preferred_element_type=F32,
        )
        acc[d, qhalf] = acc[d, qhalf] * factor + summed[:, :HD]
        total[d, qhalf] = total[d, qhalf] * factor + summed[:, HD:]
        peak[d, qhalf] = new

    def visit(d, slot, half):
        q_low = ((y + d) % 4) * 4 + zh
        k_low = y * 4 + (zh + slot) % 4
        if half == 0:
            block(d, 1, slot, 0, False)

            @pl.when(k_low < q_low)
            def _():
                block(d, 0, slot, 0, False)
        else:

            @pl.when(q_low < k_low)
            def _():
                block(d, 1, slot, 1, False)

    def visit_all(slot, half, start):
        def step(d, carry):
            visit(d, slot, half)
            return carry

        lax.fori_loop(start, 4, step, 0)

    def send_partial(half):
        def step(d, carry):
            norm = jnp.maximum(total[d, half], 1e-30)
            osend[d - 1, half] = (acc[d, half] / norm).astype(BF)
            lsend[d - 1, half, 0:2] = to_lanes(peak[d, half] * LOG2 + jnp.log2(norm))
            return carry

        lax.fori_loop(1, 4, step, 0)
        for d in (2, 1, 3):
            for copy in o_copies(d, half):
                copy.start()

    def combine(half):
        for d in (1, 2, 3):
            for copy in o_copies(d, half):
                copy.wait_recv()
        norm = jnp.maximum(total[0, half], 1e-30)
        logs = [peak[0, half] * LOG2 + jnp.log2(norm)]
        logs += [from_lanes(lrecv[s, half, 0:2]) for s in range(3)]
        top = functools.reduce(jnp.maximum, logs)
        shares = [jnp.exp2(log - top) for log in logs]
        mixed = shares[0] * (acc[0, half] / norm)
        for s in range(3):
            mixed = mixed + shares[s + 1] * orecv[s, half].astype(F32)
        out_ref[half] = (mixed / functools.reduce(jnp.add, shares)).astype(BF)

    block(0, 0, 0, 0, True)
    block(0, 1, 0, 0, False)
    block(0, 1, 0, 1, True)
    for d in (1, 2, 3):
        q_copy(d).wait_recv()
    visit_all(0, 0, 1)
    visit_all(0, 1, 1)
    for half in range(2):
        kv_arrival(3, half, 0).wait_recv()
        kv_copy(0, half, 0, True).start()
        kv_arrival(1, half, 1).wait_recv()
        kv_copy(1, half, 1, True).start()
        if half == 0:
            for sub in range(2):
                kv_copy(0, 1, sub, False).start()
                kv_copy(1, 1, 1 - sub, False).start()
        kv_arrival(3, half, 1).wait_recv()
        visit_all(3, half, 0)
        kv_arrival(1, half, 0).wait_recv()
        visit_all(1, half, 0)
        if half == 1:
            combine(0)
        kv_arrival(2, half, 0).wait_recv()
        kv_arrival(2, half, 1).wait_recv()
        visit_all(2, half, 0)
        send_partial(half)
    combine(1)
    for direction in range(2):
        for half in range(2):
            for sub in range(2):
                kv_copy(direction, half, sub, False).wait_send()
            kv_copy(direction, half, direction, True).wait_send()
    for d in (1, 2, 3):
        q_copy(d).wait_send()
        for half in range(2):
            for copy in o_copies(d, half):
                copy.wait_send()


def attend(slot_map, queries, key_vecs, value_vecs):
    dma = pltpu.SemaphoreType.DMA
    vmem = pl.BlockSpec(memory_space=pltpu.VMEM)
    return pl.pallas_call(
        attention_kernel,
        out_shape=jax.ShapeDtypeStruct((2, SPAN, HD), BF),
        in_specs=[pl.BlockSpec(memory_space=pltpu.SMEM)] + [vmem] * 3,
        out_specs=vmem,
        scratch_shapes=[
            pltpu.VMEM((4, 2, SPAN, HD), BF),
            pltpu.VMEM((4, 2, 2, SPAN, HD), BF),
            pltpu.VMEM((4, 2, SPAN, HD), F32),
            pltpu.VMEM((4, 2, SPAN, HD), F32),
            pltpu.VMEM((4, 2, SPAN, HD), F32),
            pltpu.VMEM((3, 2, SPAN, HD), BF),
            pltpu.VMEM((3, 2, 8, HD), F32),
            pltpu.VMEM((3, 2, SPAN, HD), BF),
            pltpu.VMEM((3, 2, 8, HD), F32),
            dma((3,)),
            dma((3,)),
            dma((2, 2, 3)),
            dma((4, 2, 2)),
            dma((3, 2)),
            dma((3, 2)),
            dma((3, 2)),
            dma((3, 2)),
        ],
        compiler_params=pltpu.CompilerParams(collective_id=0, has_side_effects=True),
        name="attend",
    )(slot_map, queries, key_vecs, value_vecs)


def from_everyone(x, axis):
    size = lax.axis_size(axis)
    return lax.all_to_all(jnp.broadcast_to(x[None], (size, *x.shape)), axis, 0, 0, tiled=True)


def of_everyone(x, axis):
    everything = from_everyone(x, axis)
    return jnp.sum(everything, axis=0)


def shifted(block, axis, distance):
    devices = range(lax.axis_size(axis))
    route = [(i - distance, i) for i in devices if i - distance in devices]
    return lax.ppermute(block, axis, route)


def causal_window(extended, taps_lag):
    pair_count, twice, width = extended.shape
    length = twice // 2
    tap_count = taps_lag.shape[0]
    inner = math.gcd(tap_count, 16)

    def causal_advance(block, accum):
        base = block * inner
        window = lax.dynamic_slice_in_dim(
            extended, length - base - inner + 1, length + inner - 1, 1
        ).astype(jnp.float32)
        tap_block = lax.dynamic_slice_in_dim(taps_lag, base, inner, 0).astype(jnp.float32)
        for lag in range(inner):
            offset = inner - 1 - lag
            accum = accum + tap_block[lag][None, None, :] * window[:, offset : offset + length]
        return accum

    start = jnp.zeros((pair_count, length, width), jnp.float32)
    return lax.fori_loop(0, tap_count // inner, causal_advance, start)


def on_device(
    incoming,
    queries,
    key_vecs,
    value_vecs,
    w_out,
    norm_gain,
    filters,
    filter_len,
    skip_gain,
    slot_map,
):
    tok_rows, local_width = queries.shape
    seq_rank = lax.axis_index("seq")
    seq_size = lax.axis_size("seq")
    pair_ids = lax.dynamic_slice_in_dim(slot_map, 2 * seq_rank, 2)
    low_first = pair_ids[0] < pair_ids[1]
    attention = attend(slot_map, queries, key_vecs, value_vecs).reshape(tok_rows, HD)
    incoming = incoming.reshape(2, SPAN, local_width)
    incoming = jnp.where(low_first, incoming, incoming[::-1]).reshape(tok_rows, local_width)
    projected = jnp.dot(
        lax.all_gather(attention, "mp", axis=1, tiled=True),
        w_out,
        preferred_element_type=jnp.float32,
    )
    residual = incoming.astype(jnp.float32) + projected
    square_total = of_everyone(jnp.sum(residual * residual, axis=1), "mp")
    normed = (residual * lax.rsqrt(square_total / D + EPS)[:, None] * norm_gain[None, :]).astype(
        jnp.bfloat16
    )
    tap_count = filters.shape[1]
    taps = jnp.where(
        jnp.arange(tap_count, dtype=jnp.int32)[None, :] < filter_len[:, None],
        filters,
        jnp.zeros((), filters.dtype),
    )
    taps_lag = taps.T
    own_pair = normed.reshape(2, SPAN, local_width)
    last_rank = seq_rank == seq_size - 1
    low_before = shifted(own_pair[0], "seq", 1)
    high_before = shifted(own_pair[1], "seq", -1)
    high_before = jnp.where(last_rank, own_pair[0], high_before)
    before_pair = jnp.stack([low_before, high_before])
    conv_pair = causal_window(jnp.concatenate([before_pair, own_pair], axis=1), taps_lag)
    conv_rows = conv_pair.reshape(tok_rows, local_width)
    layer_out = residual + conv_rows + skip_gain[None, :] * normed.astype(jnp.float32)
    layer_out = layer_out.astype(jnp.bfloat16).reshape(2, SPAN, local_width)
    return jnp.where(low_first, layer_out, layer_out[::-1]).reshape(tok_rows, local_width)


def solution(mesh):
    placed = (
        P("seq", "mp"),
        P("seq", "mp"),
        P("seq", "mp"),
        P("seq", "mp"),
        P(None, "mp"),
        P("mp"),
        P("mp", None),
        P("mp"),
        P("mp"),
        P(),
    )
    return jax.shard_map(
        on_device, mesh=mesh, in_specs=placed, out_specs=P("seq", "mp"), check_vma=False
    )
```

time: 313 us -> 201 us (0.64)
  waiting for transfers between devices: 200 us -> 81 us
  Pallas kernels: 0 us -> 64.5 us
  other arithmetic: 38.3 us -> 10.4 us
  matrix products: 30.1 us -> 3.58 us
  blocking collectives: 0 us -> 12.2 us
  local copies, waits for them, and re-layouts: 10.2 us -> 1.68 us
  starting transfers between devices: 14 us -> 8.59 us
    all_gather x1 -> x0, waiting for transfers between devices: 116 us -> none  [in_one_piece(): result = lax.all_gather(both, axis, axis=dim, tiled=True)]
    pallas_call x0 -> x1, Pallas kernels: none -> 64.5 us  [attend(): pl.pallas_call(attention_kernel, out_shape=jax.ShapeDtypeStruct((2, SPAN,...]
    dot_general x16 -> x0, matrix products: 26.4 us -> none  [the longest x8 14.9 us: block_update(): jnp.einsum('ths,shd->thd', weights.astype(jnp.bfloat16), value_heads, pre...]
    mul x1 -> x0, other arithmetic: 21.1 us -> none  [on_device(): jnp.repeat(slot_map, span_rows, total_repeat_length=all_rows) * span_rows]
    all_to_all x0 -> x1, blocking collectives: none -> 12.2 us  [from_everyone(): lax.all_to_all(jnp.broadcast_to(x[None], (size, *x.shape)), axis, 0, 0, t...]
    all_to_all x1 -> x0, waiting for transfers between devices: 5.72 us -> none  [from_everyone(): lax.all_to_all(jnp.broadcast_to(x[None], (size, *x.shape)), axis, 0, 0, t...]
    all_to_all x1 -> x0, starting transfers between devices: 5.37 us -> none  [from_everyone(): lax.all_to_all(jnp.broadcast_to(x[None], (size, *x.shape)), axis, 0, 0, t...]
    reduce_sum x8 -> x0, other arithmetic: 5.02 us -> none  [block_update(): total_next = total_now * factor + jnp.sum(weights, axis=2)]
  transfers between devices with their start and end apart: 5 -> 3, of which waited for: 5 -> 3; matrix products, arithmetic and copies ran while one was open for 8% -> 1% of each run, Pallas kernels for 0% -> 0%
where the time goes in v1:
time: 201 us; the launch traced here: 198 us
  waiting for transfers between devices  81 us (40%)
  Pallas kernels  64.5 us (32%)
  between operations  14.8 us (7%)
  blocking collectives  12.2 us (6%)
  other arithmetic  10.4 us (5%)
  starting transfers between devices  8.59 us (4%)
  matrix products  3.58 us (2%)
    all_gather x1, waiting for transfers between devices, on_device(): lax.all_gather(attention, 'mp', axis=1, tiled=True)  67.1 us
    pallas_call x1, Pallas kernels, attend(): pl.pallas_call(attention_kernel, out_shape=jax.ShapeDtypeStruct((2, SPAN,...  64.5 us
    ppermute x2, waiting for transfers between devices, shifted(): return lax.ppermute(block, axis, route)  13.9 us
    all_to_all x1, blocking collectives, from_everyone(): lax.all_to_all(jnp.broadcast_to(x[None], (size, *x.shape)), axis, 0, 0, t...  12.2 us
    ppermute x2, starting transfers between devices, shifted(): return lax.ppermute(block, axis, route)  8.56 us
    add x16, other arithmetic, causal_advance(): accum + tap_block[lag][None, None, :] * window[:, offset:offset + length]  7.57 us
  transfers between devices with their start and end apart: 3, of which 3 were waited for; matrix products, arithmetic and copies ran while one was open for 1% of the time, Pallas kernels for 0%

profile of v1, /device:TPU:1, one launch (start us, length us, event | category | flops | bytes accessed | tf_op | source)
XLA Modules:
  0.0 197.8 jit_solution(8905204554141429912)
XLA Ops:
  6.6 64.5 %attend.1 = bf16[2,256,128]{2,1,0:T(8,128)(2,1)} custom-call(s32[32]{0:T(128)} %slot_ref.1, bf16[512,128]{1,0:T(8,128)(2,1)} %q_ref.1, bf16[512,128]{1,0:T(8,128)(2,1)} %k_ref.1, bf16[512,128]{1,0:T(8,128)(2,1)} %v_ref.1), custom_call_target="tpu_custom_call" | custom-call | tf_op jit(solution)/shard_map/attend/pallas_call | solution.py:256
  71.1 0.7 dynamic_slice.29
  71.9 0.6 fusion.21
  73.7 1.0 reverse_select_fusion.1
  74.7 67.1 %all-gather.2.cloned.1.call-done = bf16[512,4096]{1,0:T(8,128)(2,1)} async-done(((bf16[512,128]{1,0:T(8,128)(2,1)}), bf16[512,4096]{1,0:T(8,128)(2,1)}) %all-gather.2.cloned.1.call-update) | async-done | bytes 4194320 | tf_op jit(solution)/shard_map/all_gather | solution.py:343
  141.8 3.6 %multiply_reduce_fusion = (f32[512]{0:T(512)S(1)}, f32[512,128]{1,0:T(8,128)S(1)}) fusion(bf16[512,4096]{1,0:T(8,128)(2,1)} %all-gather.2.cloned.1.call-done, bf16[4096,128]{1,0:T(8,128)(2,1)S(1)} %copy-done, bf16[512,128]{1,0:T(8,128)(2,1)S(1)} %bitcast.59), kind=kOutput, calls=%fused_computation.56 | convolution fusion | flops 537132544 | bytes 5638144 | tf_op jit(solution)/shard_map/dot_general | solution.py:342
  145.4 12.2 %all_to_all.6 = f32[32,1,512]{2,1,0:T(1,128)S(1)} all-to-all(f32[32,1,512]{2,1,0:T(1,128)S(1)} %broadcast_in_dim.9), channel_id=1, replica_groups=mesh['seq'=16,'mp'=32] {'mp'}, dimensions={0} | all-to-all | bytes 131072 | tf_op jit(solution)/shard_map/all_to_all | solution.py:287
  157.9 1.3 collective-permute-start.1
  159.3 12.6 %collective-permute-done.1 = bf16[256,128]{1,0:T(8,128)(2,1)S(1)} collective-permute-done((bf16[256,128]{1,0:T(8,128)(2,1)S(1)}, bf16[256,128]{1,0:T(8,128)(2,1)S(1)}, u32[]{:S(2)}, u32[]{:S(2)}) %collective-permute-start.1) | collective-permute-done | bytes 65568 | tf_op jit(solution)/shard_map/ppermute | solution.py:298
  172.0 7.3 %collective-permute-start = (bf16[256,128]{1,0:T(8,128)(2,1)S(1)}, bf16[256,128]{1,0:T(8,128)(2,1)S(1)}, u32[]{:S(2)}, u32[]{:S(2)}) collective-permute-start(bf16[256,128]{1,0:T(8,128)(2,1)S(1)} %get-tuple-element.187), channel_id=1, source_target_pairs={{0,32},{32,64},{64,96},{96,128},{128,160},{160,192},{192,224},{224... | collective-permute-start | bytes 196616 | tf_op jit(solution)/shard_map/ppermute | solution.py:298
  179.3 1.3 collective-permute-done
  180.6 9.5 %while.18 = (s32[]{:T(128)}, f32[2,256,128]{2,1,0:T(8,128)S(1)}, bf16[256,128]{1,0:T(8,128)(2,1)S(1)}, bf16[2,512,128]{2,1,0:T(8,128)(2,1)S(1)}, s32[]{:T(128)},...) while((s32[]{:T(128)}, f32[2,256,128]{2,1,0:T(8,128)S(1)}, ...), condition=%wide.region_3.4_spmd.clone, body=%wide.region_2.3_spmd.clone.sunk | while | flops 2234123 | bytes 5171923 | solution.py:319
  180.7 0.5 fusion.25
  181.3 0.5 fusion.25
  182.5 0.5 fusion.25
  183.1 0.5 fusion.25
  183.7 0.5 fusion.25
  184.3 0.5 fusion.25
  184.9 0.5 fusion.25
  185.5 0.5 fusion.25
  186.1 0.5 fusion.25
  186.7 0.5 fusion.25
  187.3 0.5 fusion.25
  190.3 0.7 reverse_select_fusion
  (76 shorter events, 3.9 us)
Async XLA Ops:
  6.5 135.3 %copy-start = (bf16[4096,128]{1,0:T(8,128)(2,1)S(1)}, bf16[4096,128]{1,0:T(8,128)(2,1)}, u32[]{:S(2)}) copy-start(bf16[4096,128]{1,0:T(8,128)(2,1)} %param.16) | copy-start | bytes 3145732
  6.5 151.2 %copy-start.2 = (f32[128]{0:T(128)S(1)}, f32[128]{0:T(128)}, u32[]{:S(2)}) copy-start(f32[128]{0:T(128)} %param.17) | copy-start | bytes 1540
  6.5 152.7 %copy-start.1 = (bf16[128,256]{1,0:T(8,128)(2,1)S(1)}, bf16[128,256]{1,0:T(8,128)(2,1)}, u32[]{:S(2)}) copy-start(bf16[128,256]{1,0:T(8,128)(2,1)} %param.18) | copy-start | bytes 196612
  6.5 172.7 %copy-start.3 = (s32[128]{0:T(128)S(1)}, s32[128]{0:T(128)}, u32[]{:S(2)}) copy-start(s32[128]{0:T(128)} %param.19) | copy-start | bytes 1540
  6.5 135.3 %all-gather.2.cloned.1.call-start = ((), (), s32[]{:S(2)}) async-start(), calls=%async_computation.1 | async-start | bytes 4325376 | tf_op jit(solution)/shard_map/all_gather | solution.py:343
  157.9 14.1 %collective-permute-start.1 = (bf16[256,128]{1,0:T(8,128)(2,1)S(1)}, bf16[256,128]{1,0:T(8,128)(2,1)S(1)}, u32[]{:S(2)}, u32[]{:S(2)}) collective-permute-start(bf16[256,128]{1,0:T(8,128)(2,1)S(1)} %slice.500), channel_id=1, source_target_pairs={{32,0},{64,32},{96,64},{128,96},{160,128},{192,160},{224,192},{256... | collective-permute-start | bytes 196616 | tf_op jit(solution)/shard_map/ppermute | solution.py:298
  172.0 8.6 %collective-permute-start = (bf16[256,128]{1,0:T(8,128)(2,1)S(1)}, bf16[256,128]{1,0:T(8,128)(2,1)S(1)}, u32[]{:S(2)}, u32[]{:S(2)}) collective-permute-start(bf16[256,128]{1,0:T(8,128)(2,1)S(1)} %get-tuple-element.187), channel_id=1, source_target_pairs={{0,32},{32,64},{64,96},{96,128},{128,160},{160,192},{192,224},{224... | collective-permute-start | bytes 196616 | tf_op jit(solution)/shard_map/ppermute | solution.py:298
  180.6 9.5 %copy-start.4 = (f32[128]{0:T(128)S(1)}, f32[128]{0:T(128)}, u32[]{:S(2)}) copy-start(f32[128]{0:T(128)} %param.20) | copy-start | bytes 1540
Sparse Core Ops, SparseCore 0:
  71.2 70.5 all-gather.1

commit v2 on v1

v2 whole, which is shorter than its diff:
```python
import functools
import math

import jax
import jax.numpy as jnp
from jax import lax
from jax.experimental import pallas as pl
from jax.experimental.pallas import tpu as pltpu
from jax.sharding import PartitionSpec as P

D = 4096
HD = 128
SPAN = 256
FILT = 256
EPS = 1e-05
NEG = -1e30
LOG2 = HD ** (-0.5) * math.log2(math.e)
BF = jnp.bfloat16
F32 = jnp.float32
TILE = 64


def remote(src, dst, send_sem, recv_sem, **where):
    return pltpu.make_async_remote_copy(
        src_ref=src,
        dst_ref=dst,
        send_sem=send_sem,
        recv_sem=recv_sem,
        device_id=where,
        device_id_type=pl.DeviceIdType.MESH,
    )


def greet(peers):
    barrier = pltpu.get_barrier_semaphore()
    for peer in peers:
        pl.semaphore_signal(
            barrier, inc=1, device_id=peer, device_id_type=pl.DeviceIdType.MESH
        )
    pl.semaphore_wait(barrier, len(peers))


def to_lanes(rep):
    return jnp.concatenate(
        [rep[k : k + 128].T[0:1] for k in range(0, rep.shape[0], 128)], axis=0
    )


def from_lanes(rows):
    return jnp.concatenate(
        [jnp.broadcast_to(rows[k : k + 1], (128, 128)).T for k in range(rows.shape[0])], axis=0
    )


def layer_kernel(
    slot_ref,
    q_ref,
    k_ref,
    v_ref,
    inc_ref,
    w_ref,
    gain_ref,
    filt_ref,
    flen_ref,
    skip_ref,
    out_ref,
    qb,
    kvb,
    acc,
    peak,
    total,
    osend,
    lsend,
    orecv,
    lrecv,
    gath,
    resid,
    taps,
    stat,
    stat_core,
    stat_x,
    stat_z,
    nb,
    hb,
    shift,
    conv,
    final,
    q_ssem,
    q_rsem,
    kv_ssem,
    kv_rsem,
    o_ssem,
    o_rsem,
    l_ssem,
    l_rsem,
    z_ssem,
    z_rsem,
    x_ssem,
    x_rsem,
    p_ssem,
    p_rsem,
    t_ssem,
    tc_rsem,
    tx_rsem,
    tz_rsem,
    h_ssem,
    h_rsem,
):
    rank, head = lax.axis_index("seq"), lax.axis_index("mp")
    y, zh = rank // 4, rank % 4
    along_y = [((y + d) % 4) * 4 + zh for d in range(4)]
    along_z = [y * 4 + (zh + d) % 4 for d in range(4)]
    zl, x, core = head // 8, (head // 2) % 4, head % 2
    near = jnp.where(zl == 0, 1, zl - 1)
    far = jnp.where(zl < 2, 3, 0)
    lines = [zl, near, 6 - zl - near - far, far]
    xs = [(x + d) % 4 for d in range(4)]
    partner = head + 1 - 2 * core

    def mp_of(zl_i, x_i):
        return (zl_i * 4 + x_i) * 2 + core

    gap = slot_ref[2 * rank] - slot_ref[2 * rank + 1]
    straight = jnp.full((SPAN, HD), gap, jnp.int32) < 0

    def in_order(ref, half):
        one, two = ref[0:SPAN, :].astype(F32), ref[SPAN : 2 * SPAN, :].astype(F32)
        return jnp.where(straight, (one, two)[half], (two, one)[half])

    for half in range(2):
        qb[0, half] = in_order(q_ref, half).astype(BF)
        kvb[0, half, 0] = in_order(k_ref, half).astype(BF)
        kvb[0, half, 1] = in_order(v_ref, half).astype(BF)
    greet(
        [{"seq": along_y[d]} for d in (1, 2, 3)]
        + [{"seq": along_z[d]} for d in (1, 3)]
        + [{"seq": (rank + d) % 16} for d in (1, 15)]
        + [{"mp": partner}]
        + [{"mp": mp_of(zl, xs[d])} for d in (1, 2, 3)]
        + [{"mp": mp_of(lines[k], x)} for k in (1, 2, 3)]
    )

    def kv_copy(direction, half, sub, relay):
        source = 0 if not relay else (3 if direction == 0 else 1)
        target = 2 if relay else (3 if direction == 0 else 1)
        rows = pl.ds(sub * 128, 128)
        return remote(
            kvb.at[source, half, :, rows],
            kvb.at[target, half, :, rows],
            kv_ssem.at[direction, half, 2 if relay else sub],
            kv_rsem.at[target, half, sub],
            seq=along_z[1 if direction == 0 else 3],
        )

    def kv_arrival(slot, half, sub):
        view = kvb.at[slot, half, :, pl.ds(sub * 128, 128)]
        return remote(view, view, kv_ssem.at[0, half, sub], kv_rsem.at[slot, half, sub], seq=rank)

    def q_copy(d):
        return remote(qb.at[0], qb.at[4 - d], q_ssem.at[d - 1], q_rsem.at[3 - d], seq=along_y[d])

    def o_copies(d, half):
        return (
            remote(
                osend.at[d - 1, half],
                orecv.at[3 - d, half],
                o_ssem.at[d - 1, half],
                o_rsem.at[3 - d, half],
                seq=along_y[d],
            ),
            remote(
                lsend.at[d - 1, half],
                lrecv.at[3 - d, half],
                l_ssem.at[d - 1, half],
                l_rsem.at[3 - d, half],
                seq=along_y[d],
            ),
        )

    def line_copy(half, k):
        view = gath.at[half, zl, x, core]
        return remote(
            view, view, z_ssem.at[half, k - 1], z_rsem.at[half, zl], mp=mp_of(lines[k], x)
        )

    def line_arrival(half, k):
        view = gath.at[half, lines[k], x, core]
        return remote(view, view, z_ssem.at[half, k - 1], z_rsem.at[half, lines[k]], mp=head)

    def x_copy(half, k, direction, sub, relay):
        source = xs[(3 if direction == 0 else 1) if relay else 0]
        view = gath.at[half, lines[k], source, core, pl.ds(sub * 128, 128)]
        return remote(
            view,
            view,
            x_ssem.at[half, k, direction, 2 if relay else sub],
            x_rsem.at[half, k, source, sub],
            mp=mp_of(zl, xs[1 if direction == 0 else 3]),
        )

    def x_arrival(half, k, d, sub):
        view = gath.at[half, lines[k], xs[d], core, pl.ds(sub * 128, 128)]
        return remote(view, view, x_ssem.at[half, k, 0, sub], x_rsem.at[half, k, xs[d], sub], mp=head)

    def p_copy(half, k, d):
        view = gath.at[half, lines[k], xs[d], core]
        return remote(view, view, p_ssem.at[half, k, d], p_rsem.at[half, k, d], mp=partner)

    def p_arrival(half, k, d):
        view = gath.at[half, lines[k], xs[d], 1 - core]
        return remote(view, view, p_ssem.at[half, k, d], p_rsem.at[half, k, d], mp=head)

    def core_copy(half):
        return remote(
            stat.at[half, 0], stat_core.at[half], t_ssem.at[half, 0], tc_rsem.at[half], mp=partner
        )

    def sx_copy(half, d):
        return remote(
            stat.at[half, 1],
            stat_x.at[half, 3 - d],
            t_ssem.at[half, d],
            tx_rsem.at[half, 3 - d],
            mp=mp_of(zl, xs[d]),
        )

    def sz_copy(half, k):
        return remote(
            stat.at[half, 2],
            stat_z.at[half, zl],
            t_ssem.at[half, 3 + k],
            tz_rsem.at[half, zl],
            mp=mp_of(lines[k], x),
        )

    def sz_arrival(half, k):
        view = stat_z.at[half, lines[k]]
        return remote(view, view, t_ssem.at[half, 3 + k], tz_rsem.at[half, lines[k]], mp=head)

    def h_copy(half):
        return remote(
            nb.at[half],
            hb.at[half],
            h_ssem.at[half],
            h_rsem.at[half],
            seq=(rank + (1 if half == 0 else 15)) % 16,
        )

    for sub in range(2):
        kv_copy(0, 0, sub, False).start()
        kv_copy(1, 0, 1 - sub, False).start()
    for d in (1, 3, 2):
        q_copy(d).start()

    acc[...] = jnp.zeros_like(acc)
    total[...] = jnp.zeros_like(total)
    peak[...] = jnp.full_like(peak, NEG)
    ones = jnp.ones((SPAN, HD), BF)

    def block(d, qhalf, slot, half, diagonal):
        keys, values = kvb[slot, half, 0], kvb[slot, half, 1]
        scores = lax.dot_general(
            qb[d, qhalf], keys, (((1,), (1,)), ((), ())), preferred_element_type=F32
        )
        if diagonal:
            row = lax.broadcasted_iota(jnp.int32, (SPAN, SPAN), 0)
            col = lax.broadcasted_iota(jnp.int32, (SPAN, SPAN), 1)
            scores = jnp.where(col <= row, scores, NEG)
        old = peak[d, qhalf]
        new = jnp.maximum(old, jnp.max(scores, axis=1, keepdims=True))
        weights = jnp.exp2((scores - jnp.concatenate([new, new], axis=1)) * LOG2)
        factor = jnp.exp2((old - new) * LOG2)
        summed = lax.dot_general(
            weights.astype(BF),
            jnp.concatenate([values, ones], axis=1),
            (((1,), (0,)), ((), ())),
            preferred_element_type=F32,
        )
        acc[d, qhalf] = acc[d, qhalf] * factor + summed[:, :HD]
        total[d, qhalf] = total[d, qhalf] * factor + summed[:, HD:]
        peak[d, qhalf] = new

    def visit(d, slot, half):
        q_low = ((y + d) % 4) * 4 + zh
        k_low = y * 4 + (zh + slot) % 4
        if half == 0:
            block(d, 1, slot, 0, False)

            @pl.when(k_low < q_low)
            def _():
                block(d, 0, slot, 0, False)
        else:

            @pl.when(q_low < k_low)
            def _():
                block(d, 1, slot, 1, False)

    def visit_all(slot, half, start):
        def step(d, carry):
            visit(d, slot, half)
            return carry

        lax.fori_loop(start, 4, step, 0)

    def send_partial(half):
        def step(d, carry):
            norm = jnp.maximum(total[d, half], 1e-30)
            osend[d - 1, half] = (acc[d, half] / norm).astype(BF)
            lsend[d - 1, half, 0:2] = to_lanes(peak[d, half] * LOG2 + jnp.log2(norm))
            return carry

        lax.fori_loop(1, 4, step, 0)
        for d in (2, 1, 3):
            for copy in o_copies(d, half):
                copy.start()

    def combine(half):
        for d in (1, 2, 3):
            for copy in o_copies(d, half):
                copy.wait_recv()
        norm = jnp.maximum(total[0, half], 1e-30)
        logs = [peak[0, half] * LOG2 + jnp.log2(norm)]
        logs += [from_lanes(lrecv[s, half, 0:2]) for s in range(3)]
        top = functools.reduce(jnp.maximum, logs)
        shares = [jnp.exp2(log - top) for log in logs]
        mixed = shares[0] * (acc[0, half] / norm)
        for s in range(3):
            mixed = mixed + shares[s + 1] * orecv[s, half].astype(F32)
        gath[half, zl, x, core] = (mixed / functools.reduce(jnp.add, shares)).astype(BF)

    def send_x(half, k):
        for sub in range(2):
            x_copy(half, k, 0, sub, False).start()
            x_copy(half, k, 1, 1 - sub, False).start()
        p_copy(half, k, 0).start()

    def own_out(half):
        for k in (3, 2, 1):
            line_copy(half, k).start()
        send_x(half, 0)

    def line_in(half, k):
        line_arrival(half, k).wait_recv()
        send_x(half, k)

    def x_in(half, k):
        x_arrival(half, k, 3, 0).wait_recv()
        x_copy(half, k, 0, 0, True).start()
        x_arrival(half, k, 1, 1).wait_recv()
        x_copy(half, k, 1, 1, True).start()
        x_arrival(half, k, 3, 1).wait_recv()
        p_copy(half, k, 3).start()
        x_arrival(half, k, 1, 0).wait_recv()
        p_copy(half, k, 1).start()

    def x_far(half, k):
        x_arrival(half, k, 2, 0).wait_recv()
        x_arrival(half, k, 2, 1).wait_recv()
        p_copy(half, k, 2).start()

    def project(half, k):
        for d in range(4):
            p_arrival(half, k, d).wait_recv()
        rows = jnp.concatenate(
            [gath[half, lines[k], x_i, c] for x_i in range(4) for c in range(2)], axis=1
        )
        weights = w_ref[pl.ds(pl.multiple_of(lines[k] * 1024, 1024), 1024), :]
        part = jnp.dot(rows, weights, preferred_element_type=F32)
        if k == 0:
            resid[half] = in_order(inc_ref, half) + part
        else:
            resid[half] += part

    def stat_out(half):
        square = resid[half] * resid[half]
        stat[half, 0, 0:2] = jnp.concatenate(
            [jnp.sum(square[k : k + 128].T, axis=0, keepdims=True) for k in (0, 128)], axis=0
        )
        core_copy(half).start()

    def stat_mid(half):
        core_copy(half).wait_recv()
        stat[half, 1, 0:2] = stat[half, 0, 0:2] + stat_core[half, 0:2]
        for d in (2, 1, 3):
            sx_copy(half, d).start()

    def stat_late(half):
        for d in (1, 2, 3):
            sx_copy(half, d).wait_recv()
        stat[half, 2, 0:2] = stat[half, 1, 0:2] + (
            stat_x[half, 0, 0:2] + stat_x[half, 1, 0:2] + stat_x[half, 2, 0:2]
        )
        for k in (3, 2, 1):
            sz_copy(half, k).start()

    def normalize(half):
        for k in (1, 2, 3):
            sz_arrival(half, k).wait_recv()
        whole = stat[half, 2, 0:2]
        for k in (1, 2, 3):
            whole = whole + stat_z[half, lines[k], 0:2]
        scale = from_lanes(lax.rsqrt(whole / D + EPS))
        normed = (resid[half] * scale * gain_ref[...]).astype(BF)
        nb[half] = normed
        if half == 0:

            @pl.when(rank < 15)
            def _():
                h_copy(0).start()
        else:

            @pl.when(rank > 0)
            def _():
                h_copy(1).start()

        wide = normed.astype(F32)
        resid[half] += skip_ref[...] * wide
        for s in range(8):
            shift[half, s, SPAN + s : 2 * SPAN + s, :] = wide

    def lags(half, top, begin, end, start):
        def step(a, run):
            eight = taps[pl.ds(pl.multiple_of(a * 8, 8), 8), :]
            rows = pl.ds(pl.multiple_of(SPAN + top - a * 8, 8), TILE)
            for s in range(8):
                run = run + eight[s : s + 1] * shift[half, s, rows, :]
            return run

        return lax.fori_loop(begin, end, step, start)

    def conv_own(half):
        for top in range(TILE, SPAN, TILE):
            conv[half, top : top + TILE, :] = lags(
                half, top, 0, top // 8, jnp.zeros((TILE, HD), F32)
            )

    def conv_rest(half):
        edge = rank == (0 if half == 0 else 15)

        @pl.when(edge)
        def _():
            hb[half] = jnp.zeros((SPAN, HD), BF) if half == 0 else nb[0]

        @pl.when(jnp.logical_not(edge))
        def _():
            h_copy(half).wait_recv()

        before = hb[half].astype(F32)
        for s in range(8):
            shift[half, s, s : SPAN + s, :] = before
        for top in range(0, SPAN, TILE):
            begin = jnp.zeros((TILE, HD), F32) if top == 0 else conv[half, top : top + TILE, :]
            final[half, top : top + TILE, :] = resid[half, top : top + TILE, :] + lags(
                half, top, top // 8, FILT // 8, begin
            )

    block(0, 0, 0, 0, True)
    block(0, 1, 0, 0, False)
    block(0, 1, 0, 1, True)
    lag = lax.broadcasted_iota(jnp.int32, (FILT, HD), 0)
    turned = jnp.concatenate(
        [filt_ref[:, k : k + 128].astype(F32).T for k in (0, 128)], axis=0
    )
    taps[...] = jnp.where(lag < flen_ref[...], turned, 0.0)
    for d in (1, 2, 3):
        q_copy(d).wait_recv()
    visit_all(0, 0, 1)
    visit_all(0, 1, 1)

    kv_arrival(3, 0, 0).wait_recv()
    kv_copy(0, 0, 0, True).start()
    kv_arrival(1, 0, 1).wait_recv()
    kv_copy(1, 0, 1, True).start()
    for sub in range(2):
        kv_copy(0, 1, sub, False).start()
        kv_copy(1, 1, 1 - sub, False).start()
    kv_arrival(3, 0, 1).wait_recv()
    visit_all(3, 0, 0)
    kv_arrival(1, 0, 0).wait_recv()
    visit_all(1, 0, 0)
    kv_arrival(2, 0, 0).wait_recv()
    kv_arrival(2, 0, 1).wait_recv()
    visit_all(2, 0, 0)
    send_partial(0)

    kv_arrival(3, 1, 0).wait_recv()
    kv_copy(0, 1, 0, True).start()
    kv_arrival(1, 1, 1).wait_recv()
    kv_copy(1, 1, 1, True).start()
    combine(0)
    own_out(0)
    kv_arrival(3, 1, 1).wait_recv()
    visit_all(3, 1, 0)
    line_in(0, 1)
    x_in(0, 0)
    kv_arrival(1, 1, 0).wait_recv()
    visit_all(1, 1, 0)
    line_in(0, 2)
    x_in(0, 1)
    kv_arrival(2, 1, 0).wait_recv()
    kv_arrival(2, 1, 1).wait_recv()
    visit_all(2, 1, 0)
    send_partial(1)
    line_in(0, 3)
    x_far(0, 0)
    project(0, 0)
    x_in(0, 2)
    combine(1)
    own_out(1)
    x_far(0, 1)
    project(0, 1)
    x_in(0, 3)
    line_in(1, 1)
    x_far(0, 2)
    project(0, 2)
    x_in(1, 0)
    x_far(0, 3)
    line_in(1, 2)
    project(0, 3)
    stat_out(0)
    x_in(1, 1)
    line_in(1, 3)
    stat_mid(0)
    x_far(1, 0)
    project(1, 0)
    x_in(1, 2)
    stat_late(0)
    x_far(1, 1)
    project(1, 1)
    x_in(1, 3)
    x_far(1, 2)
    project(1, 2)
    normalize(0)
    x_far(1, 3)
    project(1, 3)
    stat_out(1)
    conv_own(0)
    stat_mid(1)
    conv_rest(0)
    stat_late(1)
    normalize(1)
    conv_own(1)
    conv_rest(1)
    low, high = final[0], final[1]
    out_ref[0:SPAN, :] = jnp.where(straight, low, high).astype(BF)
    out_ref[SPAN : 2 * SPAN, :] = jnp.where(straight, high, low).astype(BF)

    for half in range(2):
        for direction in range(2):
            for sub in range(2):
                kv_copy(direction, half, sub, False).wait_send()
            kv_copy(direction, half, direction, True).wait_send()
            for k in range(4):
                for sub in range(2):
                    x_copy(half, k, direction, sub, False).wait_send()
                x_copy(half, k, direction, direction, True).wait_send()
        for k in range(4):
            for d in range(4):
                p_copy(half, k, d).wait_send()
        core_copy(half).wait_send()
        for k in (1, 2, 3):
            for copy in o_copies(k, half):
                copy.wait_send()
            line_copy(half, k).wait_send()
            sx_copy(half, k).wait_send()
            sz_copy(half, k).wait_send()

        @pl.when(rank != (15 if half == 0 else 0))
        def _():
            h_copy(half).wait_send()

    for d in (1, 2, 3):
        q_copy(d).wait_send()


def on_device(
    incoming,
    queries,
    key_vecs,
    value_vecs,
    w_out,
    norm_gain,
    filters,
    filter_len,
    skip_gain,
    slot_map,
):
    dma = pltpu.SemaphoreType.DMA
    vmem = pl.BlockSpec(memory_space=pltpu.VMEM)
    return pl.pallas_call(
        layer_kernel,
        out_shape=jax.ShapeDtypeStruct(queries.shape, BF),
        in_specs=[pl.BlockSpec(memory_space=pltpu.SMEM)] + [vmem] * 9,
        out_specs=vmem,
        scratch_shapes=[
            pltpu.VMEM((4, 2, SPAN, HD), BF),
            pltpu.VMEM((4, 2, 2, SPAN, HD), BF),
            pltpu.VMEM((4, 2, SPAN, HD), F32),
            pltpu.VMEM((4, 2, SPAN, HD), F32),
            pltpu.VMEM((4, 2, SPAN, HD), F32),
            pltpu.VMEM((3, 2, SPAN, HD), BF),
            pltpu.VMEM((3, 2, 8, HD), F32),
            pltpu.VMEM((3, 2, SPAN, HD), BF),
            pltpu.VMEM((3, 2, 8, HD), F32),
            pltpu.VMEM((2, 4, 4, 2, SPAN, HD), BF),
            pltpu.VMEM((2, SPAN, HD), F32),
            pltpu.VMEM((FILT, HD), F32),
            pltpu.VMEM((2, 3, 8, HD), F32),
            pltpu.VMEM((2, 8, HD), F32),
            pltpu.VMEM((2, 3, 8, HD), F32),
            pltpu.VMEM((2, 4, 8, HD), F32),
            pltpu.VMEM((2, SPAN, HD), BF),
            pltpu.VMEM((2, SPAN, HD), BF),
            pltpu.VMEM((2, 8, 2 * SPAN + 8, HD), F32),
            pltpu.VMEM((2, SPAN, HD), F32),
            pltpu.VMEM((2, SPAN, HD), F32),
            dma((3,)),
            dma((3,)),
            dma((2, 2, 3)),
            dma((4, 2, 2)),
            dma((3, 2)),
            dma((3, 2)),
            dma((3, 2)),
            dma((3, 2)),
            dma((2, 3)),
            dma((2, 4)),
            dma((2, 4, 2, 3)),
            dma((2, 4, 4, 2)),
            dma((2, 4, 4)),
            dma((2, 4, 4)),
            dma((2, 7)),
            dma((2,)),
            dma((2, 3)),
            dma((2, 4)),
            dma((2,)),
            dma((2,)),
        ],
        compiler_params=pltpu.CompilerParams(collective_id=0, has_side_effects=True),
        name="layer",
    )(
        slot_map,
        queries,
        key_vecs,
        value_vecs,
        incoming,
        w_out,
        norm_gain.reshape(1, HD),
        filters,
        filter_len.reshape(1, HD),
        skip_gain.reshape(1, HD),
    )


def solution(mesh):
    placed = (
        P("seq", "mp"),
        P("seq", "mp"),
        P("seq", "mp"),
        P("seq", "mp"),
        P(None, "mp"),
        P("mp"),
        P("mp", None),
        P("mp"),
        P("mp"),
        P(),
    )
    return jax.shard_map(
        on_device, mesh=mesh, in_specs=placed, out_specs=P("seq", "mp"), check_vma=False
    )
```

time: 201 us -> 115 us (0.57); the launches traced: 198 us -> 115 us
  waiting for transfers between devices: 81 us -> 0 us
  Pallas kernels: 64.5 us -> 113 us
  between operations: 14.8 us -> 0.01 us
  blocking collectives: 12.2 us -> 0 us
  other arithmetic: 10.4 us -> 0 us
  starting transfers between devices: 8.59 us -> 0 us
  matrix products: 3.58 us -> 0 us
    all_gather x1 -> x0, waiting for transfers between devices: 67.1 us -> none  [on_device(): lax.all_gather(attention, 'mp', axis=1, tiled=True)]
    pallas_call x1, Pallas kernels: 64.5 us -> 113 us  [on_device(): pl.pallas_call(layer_kernel, out_shape=jax.ShapeDtypeStruct(queries.shape...]
    ppermute x2 -> x0, waiting for transfers between devices: 13.9 us -> none  [shifted(): return lax.ppermute(block, axis, route)]
    all_to_all x1 -> x0, blocking collectives: 12.2 us -> none  [from_everyone(): lax.all_to_all(jnp.broadcast_to(x[None], (size, *x.shape)), axis, 0, 0, t...]
    ppermute x2 -> x0, starting transfers between devices: 8.56 us -> none  [shifted(): return lax.ppermute(block, axis, route)]
    add x16 -> x0, other arithmetic: 7.57 us -> none  [causal_advance(): accum + tap_block[lag][None, None, :] * window[:, offset:offset + length]]
    dot_general x1 -> x0, matrix products: 3.58 us -> none  [on_device(): jnp.dot(lax.all_gather(attention, 'mp', axis=1, tiled=True), w_out, prefe...]
  transfers between devices with their start and end apart: 3 -> 0, of which waited for: 3 -> 0; matrix products, arithmetic and copies ran while one was open for 1% -> 0% of each run, Pallas kernels for 0% -> 0%
where the time goes in v2:
time: 115 us
  Pallas kernels  113 us (98%)
  local copies, waits for them, and re-layouts  1.57 us (1%)
    pallas_call x1, Pallas kernels, on_device(): pl.pallas_call(layer_kernel, out_shape=jax.ShapeDtypeStruct(queries.shape...  113 us

profile of v2, /device:TPU:1, one launch (start us, length us, event | category | flops | bytes accessed | tf_op | source)
XLA Modules:
  0.0 114.5 jit_solution(8108442412438204017)
XLA Ops:
  0.0 112.9 %layer.1 = bf16[512,128]{1,0:T(8,128)(2,1)} custom-call(s32[32]{0:T(128)} %slot_ref.1, bf16[512,128]{1,0:T(8,128)(2,1)} %q_ref.1, bf16[512,128]{1,0:T(8,128)(2,1)} %k_ref.1, bf16[512,128]{1,0:T(8,128)(2,1)} %v_ref.1, bf16[512,128]{1,0:T(8,128)(2,1)} %inc_ref.1, bf16[4096,128]{1,0:T(8,128)(2,1)} %w_ref.1, f32[1,128]{1,0:T(1,128)} %bitcast.3, ...), custom_call_target="tpu_custom_call" | custom-call | tf_op jit(solution)/shard_map/layer/pallas_call | solution.py:590
  112.9 1.6 %copy.12 = bf16[512,128]{1,0:T(8,128)(2,1)} copy(bf16[512,128]{1,0:T(8,128)(2,1)} %layer.1) | data formatting | bytes 262144

commit v3 on v2

--- a/solution.py
+++ b/solution.py
@@ -74,14 +74,19 @@
     orecv,
     lrecv,
     gath,
+    w_pair,
+    sums,
+    part_send,
+    part_recv,
     resid,
     taps,
     stat,
-    stat_core,
     stat_x,
     stat_z,
-    nb,
+    rb,
     hb,
+    scales,
+    hs,
     shift,
     conv,
     final,
@@ -99,12 +104,16 @@
     x_rsem,
     p_ssem,
     p_rsem,
-    t_ssem,
-    tc_rsem,
+    w_ssem,
+    w_rsem,
+    tx_ssem,
     tx_rsem,
+    tz_ssem,
     tz_rsem,
     h_ssem,
     h_rsem,
+    s_ssem,
+    s_rsem,
 ):
     rank, head = lax.axis_index("seq"), lax.axis_index("mp")
     y, zh = rank // 4, rank % 4
@@ -117,8 +126,8 @@
     xs = [(x + d) % 4 for d in range(4)]
     partner = head + 1 - 2 * core
 
-    def mp_of(zl_i, x_i):
-        return (zl_i * 4 + x_i) * 2 + core
+    def mp_of(zl_i, x_i, core_i=core):
+        return (zl_i * 4 + x_i) * 2 + core_i
 
     gap = slot_ref[2 * rank] - slot_ref[2 * rank + 1]
     straight = jnp.full((SPAN, HD), gap, jnp.int32) < 0
@@ -137,6 +146,7 @@
         + [{"seq": (rank + d) % 16} for d in (1, 15)]
         + [{"mp": partner}]
         + [{"mp": mp_of(zl, xs[d])} for d in (1, 2, 3)]
+        + [{"mp": mp_of(zl, xs[d], 1 - core)} for d in (1, 2, 3)]
         + [{"mp": mp_of(lines[k], x)} for k in (1, 2, 3)]
     )
 
@@ -178,18 +188,18 @@
         )
 
     def line_copy(half, k):
-        view = gath.at[half, zl, x, core]
+        view = gath.at[half, zl, x]
         return remote(
             view, view, z_ssem.at[half, k - 1], z_rsem.at[half, zl], mp=mp_of(lines[k], x)
         )
 
     def line_arrival(half, k):
-        view = gath.at[half, lines[k], x, core]
+        view = gath.at[half, lines[k], x]
         return remote(view, view, z_ssem.at[half, k - 1], z_rsem.at[half, lines[k]], mp=head)
 
     def x_copy(half, k, direction, sub, relay):
         source = xs[(3 if direction == 0 else 1) if relay else 0]
-        view = gath.at[half, lines[k], source, core, pl.ds(sub * 128, 128)]
+        view = gath.at[half, lines[k], source, pl.ds(sub * 128, 128)]
         return remote(
             view,
             view,
@@ -199,50 +209,60 @@
         )
 
     def x_arrival(half, k, d, sub):
-        view = gath.at[half, lines[k], xs[d], core, pl.ds(sub * 128, 128)]
+        view = gath.at[half, lines[k], xs[d], pl.ds(sub * 128, 128)]
         return remote(view, view, x_ssem.at[half, k, 0, sub], x_rsem.at[half, k, xs[d], sub], mp=head)
 
-    def p_copy(half, k, d):
-        view = gath.at[half, lines[k], xs[d], core]
-        return remote(view, view, p_ssem.at[half, k, d], p_rsem.at[half, k, d], mp=partner)
-
-    def p_arrival(half, k, d):
-        view = gath.at[half, lines[k], xs[d], 1 - core]
-        return remote(view, view, p_ssem.at[half, k, d], p_rsem.at[half, k, d], mp=head)
-
-    def core_copy(half):
-        return remote(
-            stat.at[half, 0], stat_core.at[half], t_ssem.at[half, 0], tc_rsem.at[half], mp=partner
-        )
-
-    def sx_copy(half, d):
+    w_copy = remote(w_ref.at[:, 1 - core], w_pair, w_ssem.at[0], w_rsem.at[0], mp=partner)
+
+    def part_copy(half):
+        return remote(
+            part_send.at[half], part_recv.at[half], p_ssem.at[half], p_rsem.at[half], mp=partner
+        )
+
+    plane = [(d, c) for d in (2, 1, 3, 0) for c in (0, 1) if (d, c) != (0, 0)]
+
+    def sx_copy(half, d, flip):
+        return remote(
+            stat.at[half, 0],
+            stat_x.at[half, x * 2 + core],
+            tx_ssem.at[half, d * 2 + flip],
+            tx_rsem.at[half, x * 2 + core],
+            mp=mp_of(zl, xs[d], core + flip - 2 * core * flip),
+        )
+
+    def sx_arrival(half, d, flip):
+        spot = xs[d] * 2 + core + flip - 2 * core * flip
+        view = stat_x.at[half, spot]
+        return remote(view, view, tx_ssem.at[half, 0], tx_rsem.at[half, spot], mp=head)
+
+    def sz_copy(half, k):
         return remote(
             stat.at[half, 1],
-            stat_x.at[half, 3 - d],
-            t_ssem.at[half, d],
-            tx_rsem.at[half, 3 - d],
-            mp=mp_of(zl, xs[d]),
-        )
-
-    def sz_copy(half, k):
-        return remote(
-            stat.at[half, 2],
             stat_z.at[half, zl],
-            t_ssem.at[half, 3 + k],
+            tz_ssem.at[half, k],
             tz_rsem.at[half, zl],
             mp=mp_of(lines[k], x),
         )
 
     def sz_arrival(half, k):
         view = stat_z.at[half, lines[k]]
-        return remote(view, view, t_ssem.at[half, 3 + k], tz_rsem.at[half, lines[k]], mp=head)
+        return remote(view, view, tz_ssem.at[half, k], tz_rsem.at[half, lines[k]], mp=head)
 
     def h_copy(half):
         return remote(
-            nb.at[half],
+            rb.at[half],
             hb.at[half],
             h_ssem.at[half],
             h_rsem.at[half],
+            seq=(rank + (1 if half == 0 else 15)) % 16,
+        )
+
+    def s_copy(half):
+        return remote(
+            scales.at[half],
+            hs.at[half],
+            s_ssem.at[half],
+            s_rsem.at[half],
             seq=(rank + (1 if half == 0 else 15)) % 16,
         )
 
@@ -326,16 +346,15 @@
         mixed = shares[0] * (acc[0, half] / norm)
         for s in range(3):
             mixed = mixed + shares[s + 1] * orecv[s, half].astype(F32)
-        gath[half, zl, x, core] = (mixed / functools.reduce(jnp.add, shares)).astype(BF)
+        gath[half, zl, x] = (mixed / functools.reduce(jnp.add, shares)).astype(BF)
 
     def send_x(half, k):
         for sub in range(2):
             x_copy(half, k, 0, sub, False).start()
             x_copy(half, k, 1, 1 - sub, False).start()
-        p_copy(half, k, 0).start()
 
     def own_out(half):
-        for k in (3, 2, 1):
+        for k in (1, 2, 3):
             line_copy(half, k).start()
         send_x(half, 0)
 
@@ -348,71 +367,75 @@
         x_copy(half, k, 0, 0, True).start()
         x_arrival(half, k, 1, 1).wait_recv()
         x_copy(half, k, 1, 1, True).start()
+
+    def project(half, k):
         x_arrival(half, k, 3, 1).wait_recv()
-        p_copy(half, k, 3).start()
         x_arrival(half, k, 1, 0).wait_recv()
-        p_copy(half, k, 1).start()
-
-    def x_far(half, k):
         x_arrival(half, k, 2, 0).wait_recv()
         x_arrival(half, k, 2, 1).wait_recv()
-        p_copy(half, k, 2).start()
-
-    def project(half, k):
-        for d in range(4):
-            p_arrival(half, k, d).wait_recv()
-        rows = jnp.concatenate(
-            [gath[half, lines[k], x_i, c] for x_i in range(4) for c in range(2)], axis=1
-        )
-        weights = w_ref[pl.ds(pl.multiple_of(lines[k] * 1024, 1024), 1024), :]
+        rows = jnp.concatenate([gath[half, lines[k], x_i] for x_i in range(4)], axis=1)
+        weights = jnp.concatenate(
+            [
+                jnp.concatenate(
+                    [w_ref[lines[k] * 4 + x_i, core], w_pair[lines[k] * 4 + x_i]], axis=1
+                )
+                for x_i in range(4)
+            ],
+            axis=0,
+        )
         part = jnp.dot(rows, weights, preferred_element_type=F32)
         if k == 0:
-            resid[half] = in_order(inc_ref, half) + part
+            sums[half] = part
+        elif k < 3:
+            sums[half] += part
         else:
-            resid[half] += part
-
-    def stat_out(half):
-        square = resid[half] * resid[half]
+            both = sums[half] + part
+            part_send[half] = both[:, HD:]
+            part_copy(half).start()
+            resid[half] = in_order(inc_ref, half) + both[:, :HD]
+
+    def finish(half):
+        part_copy(half).wait_recv()
+        whole = resid[half] + part_recv[half]
+        square = whole * whole
         stat[half, 0, 0:2] = jnp.concatenate(
             [jnp.sum(square[k : k + 128].T, axis=0, keepdims=True) for k in (0, 128)], axis=0
         )
-        core_copy(half).start()
-
-    def stat_mid(half):
-        core_copy(half).wait_recv()
-        stat[half, 1, 0:2] = stat[half, 0, 0:2] + stat_core[half, 0:2]
-        for d in (2, 1, 3):
-            sx_copy(half, d).start()
+        for d, flip in plane:
+            sx_copy(half, d, flip).start()
+        resid[half] = whole
+        rb[half] = whole.astype(BF)
+
+        @pl.when(rank != (15 if half == 0 else 0))
+        def _():
+            h_copy(half).start()
 
     def stat_late(half):
-        for d in (1, 2, 3):
-            sx_copy(half, d).wait_recv()
-        stat[half, 2, 0:2] = stat[half, 1, 0:2] + (
-            stat_x[half, 0, 0:2] + stat_x[half, 1, 0:2] + stat_x[half, 2, 0:2]
-        )
+        for d, flip in plane:
+            sx_arrival(half, d, flip).wait_recv()
+        stat_x[half, x * 2 + core, 0:2] = stat[half, 0, 0:2]
+        run = stat_x[half, 0, 0:2]
+        for k in range(1, 8):
+            run = run + stat_x[half, k, 0:2]
+        stat[half, 1, 0:2] = run
         for k in (3, 2, 1):
             sz_copy(half, k).start()
 
     def normalize(half):
         for k in (1, 2, 3):
             sz_arrival(half, k).wait_recv()
-        whole = stat[half, 2, 0:2]
+        whole = stat[half, 1, 0:2]
         for k in (1, 2, 3):
             whole = whole + stat_z[half, lines[k], 0:2]
-        scale = from_lanes(lax.rsqrt(whole / D + EPS))
+        lane_scale = lax.rsqrt(whole / D + EPS)
+        scales[half, 0:2] = lane_scale
+
+        @pl.when(rank != (15 if half == 0 else 0))
+        def _():
+            s_copy(half).start()
+
+        scale = from_lanes(lane_scale)
         normed = (resid[half] * scale * gain_ref[...]).astype(BF)
-        nb[half] = normed
-        if half == 0:
-
-            @pl.when(rank < 15)
-            def _():
-                h_copy(0).start()
-        else:
-
-            @pl.when(rank > 0)
-            def _():
-                h_copy(1).start()
-
         wide = normed.astype(F32)
         resid[half] += skip_ref[...] * wide
         for s in range(8):
@@ -439,13 +462,16 @@
 
         @pl.when(edge)
         def _():
-            hb[half] = jnp.zeros((SPAN, HD), BF) if half == 0 else nb[0]
+            hb[half] = jnp.zeros((SPAN, HD), BF) if half == 0 else rb[0]
+            hs[half, 0:2] = jnp.zeros((2, HD), F32) if half == 0 else scales[0, 0:2]
 
         @pl.when(jnp.logical_not(edge))
         def _():
             h_copy(half).wait_recv()
-
-        before = hb[half].astype(F32)
+            s_copy(half).wait_recv()
+
+        rows = hb[half].astype(F32) * from_lanes(hs[half, 0:2]) * gain_ref[...]
+        before = rows.astype(BF).astype(F32)
         for s in range(8):
             shift[half, s, s : SPAN + s, :] = before
         for top in range(0, SPAN, TILE):
@@ -454,6 +480,17 @@
                 half, top, top // 8, FILT // 8, begin
             )
 
+    def low_relay(half):
+        kv_arrival(3, half, 0).wait_recv()
+        kv_copy(0, half, 0, True).start()
+        kv_arrival(1, half, 1).wait_recv()
+        kv_copy(1, half, 1, True).start()
+
+    def send_high(sub):
+        kv_copy(0, 1, sub, False).start()
+        kv_copy(1, 1, 1 - sub, False).start()
+
+    w_copy.start()
     block(0, 0, 0, 0, True)
     block(0, 1, 0, 0, False)
     block(0, 1, 0, 1, True)
@@ -465,77 +502,59 @@
     for d in (1, 2, 3):
         q_copy(d).wait_recv()
     visit_all(0, 0, 1)
+    low_relay(0)
     visit_all(0, 1, 1)
-
-    kv_arrival(3, 0, 0).wait_recv()
-    kv_copy(0, 0, 0, True).start()
-    kv_arrival(1, 0, 1).wait_recv()
-    kv_copy(1, 0, 1, True).start()
-    for sub in range(2):
-        kv_copy(0, 1, sub, False).start()
-        kv_copy(1, 1, 1 - sub, False).start()
     kv_arrival(3, 0, 1).wait_recv()
+    send_high(0)
     visit_all(3, 0, 0)
     kv_arrival(1, 0, 0).wait_recv()
+    send_high(1)
     visit_all(1, 0, 0)
     kv_arrival(2, 0, 0).wait_recv()
     kv_arrival(2, 0, 1).wait_recv()
     visit_all(2, 0, 0)
     send_partial(0)
-
-    kv_arrival(3, 1, 0).wait_recv()
-    kv_copy(0, 1, 0, True).start()
-    kv_arrival(1, 1, 1).wait_recv()
-    kv_copy(1, 1, 1, True).start()
+    low_relay(1)
     combine(0)
     own_out(0)
+    w_copy.wait_recv()
+    x_in(0, 0)
     kv_arrival(3, 1, 1).wait_recv()
     visit_all(3, 1, 0)
     line_in(0, 1)
-    x_in(0, 0)
     kv_arrival(1, 1, 0).wait_recv()
     visit_all(1, 1, 0)
     line_in(0, 2)
     x_in(0, 1)
+    line_in(0, 3)
     kv_arrival(2, 1, 0).wait_recv()
     kv_arrival(2, 1, 1).wait_recv()
     visit_all(2, 1, 0)
     send_partial(1)
-    line_in(0, 3)
-    x_far(0, 0)
     project(0, 0)
     x_in(0, 2)
+    project(0, 1)
     combine(1)
     own_out(1)
-    x_far(0, 1)
-    project(0, 1)
     x_in(0, 3)
+    project(0, 2)
     line_in(1, 1)
-    x_far(0, 2)
-    project(0, 2)
     x_in(1, 0)
-    x_far(0, 3)
     line_in(1, 2)
     project(0, 3)
-    stat_out(0)
+    line_in(1, 3)
     x_in(1, 1)
-    line_in(1, 3)
-    stat_mid(0)
-    x_far(1, 0)
+    finish(0)
     project(1, 0)
     x_in(1, 2)
     stat_late(0)
-    x_far(1, 1)
     project(1, 1)
     x_in(1, 3)
-    x_far(1, 2)
+    normalize(0)
     project(1, 2)
-    normalize(0)
-    x_far(1, 3)
     project(1, 3)
-    stat_out(1)
     conv_own(0)
-    stat_mid(1)
+    finish(1)
     conv_rest(0)
     stat_late(1)
     normalize(1)
@@ -554,21 +573,21 @@
                 for sub in range(2):
                     x_copy(half, k, direction, sub, False).wait_send()
                 x_copy(half, k, direction, direction, True).wait_send()
-        for k in range(4):
-            for d in range(4):
-                p_copy(half, k, d).wait_send()
-        core_copy(half).wait_send()
+        part_copy(half).wait_send()
+        for d, flip in plane:
+            sx_copy(half, d, flip).wait_send()
         for k in (1, 2, 3):
             for copy in o_copies(k, half):
                 copy.wait_send()
             line_copy(half, k).wait_send()
-            sx_copy(half, k).wait_send()
             sz_copy(half, k).wait_send()
 
         @pl.when(rank != (15 if half == 0 else 0))
         def _():
             h_copy(half).wait_send()
-
+            s_copy(half).wait_send()
+
+    w_copy.wait_send()
     for d in (1, 2, 3):
         q_copy(d).wait_send()
 
@@ -602,15 +621,20 @@
             pltpu.VMEM((3, 2, 8, HD), F32),
             pltpu.VMEM((3, 2, SPAN, HD), BF),
             pltpu.VMEM((3, 2, 8, HD), F32),
-            pltpu.VMEM((2, 4, 4, 2, SPAN, HD), BF),
+            pltpu.VMEM((2, 4, 4, SPAN, HD), BF),
+            pltpu.VMEM((16, HD, HD), BF),
+            pltpu.VMEM((2, SPAN, 2 * HD), F32),
+            pltpu.VMEM((2, SPAN, HD), F32),
+            pltpu.VMEM((2, SPAN, HD), F32),
             pltpu.VMEM((2, SPAN, HD), F32),
             pltpu.VMEM((FILT, HD), F32),
-            pltpu.VMEM((2, 3, 8, HD), F32),
-            pltpu.VMEM((2, 8, HD), F32),
-            pltpu.VMEM((2, 3, 8, HD), F32),
+            pltpu.VMEM((2, 2, 8, HD), F32),
+            pltpu.VMEM((2, 8, 8, HD), F32),
             pltpu.VMEM((2, 4, 8, HD), F32),
             pltpu.VMEM((2, SPAN, HD), BF),
             pltpu.VMEM((2, SPAN, HD), BF),
+            pltpu.VMEM((2, 8, HD), F32),
+            pltpu.VMEM((2, 8, HD), F32),
             pltpu.VMEM((2, 8, 2 * SPAN + 8, HD), F32),
             pltpu.VMEM((2, SPAN, HD), F32),
             pltpu.VMEM((2, SPAN, HD), F32),
@@ -626,12 +650,16 @@
             dma((2, 4)),
             dma((2, 4, 2, 3)),
             dma((2, 4, 4, 2)),
-            dma((2, 4, 4)),
-            dma((2, 4, 4)),
-            dma((2, 7)),
             dma((2,)),
-            dma((2, 3)),
+            dma((2,)),
+            dma((1,)),
+            dma((1,)),
+            dma((2, 8)),
+            dma((2, 8)),
             dma((2, 4)),
+            dma((2, 4)),
+            dma((2,)),
+            dma((2,)),
             dma((2,)),
             dma((2,)),
         ],
@@ -643,7 +671,7 @@
         key_vecs,
         value_vecs,
         incoming,
-        w_out,
+        w_out.reshape(16, 2, HD, HD),
         norm_gain.reshape(1, HD),
         filters,
         filter_len.reshape(1, HD),

time: 115 us -> 105 us (0.913); the launches traced: 115 us -> 103 us
  Pallas kernels: 113 us -> 102 us
    pallas_call x1, Pallas kernels: 113 us -> 102 us  [on_device(): pl.pallas_call(layer_kernel, out_shape=jax.ShapeDtypeStruct(queries.shape...]
where the time goes in v3:
time: 105 us; the launch traced here: 103 us
  Pallas kernels  102 us (97%)
  local copies, waits for them, and re-layouts  1.57 us (1%)
    pallas_call x1, Pallas kernels, on_device(): pl.pallas_call(layer_kernel, out_shape=jax.ShapeDtypeStruct(queries.shape...  102 us

profile of v3, /device:TPU:1, one launch (start us, length us, event | category | flops | bytes accessed | tf_op | source)
XLA Modules:
  0.0 103.3 jit_solution(8636753230111486023)
XLA Ops:
  0.0 101.7 %layer.1 = bf16[512,128]{1,0:T(8,128)(2,1)} custom-call(s32[32]{0:T(128)} %slot_ref.1, bf16[512,128]{1,0:T(8,128)(2,1)} %q_ref.1, bf16[512,128]{1,0:T(8,128)(2,1)} %k_ref.1, bf16[512,128]{1,0:T(8,128)(2,1)} %v_ref.1, bf16[512,128]{1,0:T(8,128)(2,1)} %inc_ref.1, bf16[16,2,128,128]{3,2,1,0:T(8,128)(2,1)} %bitcast.4, f32[1,128]{1,0:T(1,128)} %bitcast.5, ...), custom_call_target="tpu_custom_call" | custom-call | tf_op jit(solution)/shard_map/layer/pallas_call | solution.py:609
  101.7 1.6 %copy.12 = bf16[512,128]{1,0:T(8,128)(2,1)} copy(bf16[512,128]{1,0:T(8,128)(2,1)} %layer.1) | data formatting | bytes 262144

commit v4 on v3

--- a/solution.py
+++ b/solution.py
@@ -31,15 +31,6 @@
     )
 
 
-def greet(peers):
-    barrier = pltpu.get_barrier_semaphore()
-    for peer in peers:
-        pl.semaphore_signal(
-            barrier, inc=1, device_id=peer, device_id_type=pl.DeviceIdType.MESH
-        )
-    pl.semaphore_wait(barrier, len(peers))
-
-
 def to_lanes(rep):
     return jnp.concatenate(
         [rep[k : k + 128].T[0:1] for k in range(0, rep.shape[0], 128)], axis=0
@@ -54,16 +45,25 @@
 
 def layer_kernel(
     slot_ref,
+    q_hbm,
+    k_hbm,
+    v_hbm,
+    w_hbm,
+    inc_hbm,
+    filt_hbm,
+    gain_hbm,
+    flen_hbm,
+    skip_hbm,
+    out_ref,
     q_ref,
     k_ref,
     v_ref,
+    w_ref,
     inc_ref,
-    w_ref,
+    filt_ref,
     gain_ref,
-    filt_ref,
     flen_ref,
     skip_ref,
-    out_ref,
     qb,
     kvb,
     acc,
@@ -114,7 +114,10 @@
     h_rsem,
     s_ssem,
     s_rsem,
+    in_sem,
 ):
+    arrays = (q_hbm, k_hbm, v_hbm, w_hbm, inc_hbm, filt_hbm, gain_hbm, flen_hbm, skip_hbm)
+    held = (q_ref, k_ref, v_ref, w_ref, inc_ref, filt_ref, gain_ref, flen_ref, skip_ref)
     rank, head = lax.axis_index("seq"), lax.axis_index("mp")
     y, zh = rank // 4, rank % 4
     along_y = [((y + d) % 4) * 4 + zh for d in range(4)]
@@ -129,18 +132,7 @@
     def mp_of(zl_i, x_i, core_i=core):
         return (zl_i * 4 + x_i) * 2 + core_i
 
-    gap = slot_ref[2 * rank] - slot_ref[2 * rank + 1]
-    straight = jnp.full((SPAN, HD), gap, jnp.int32) < 0
-
-    def in_order(ref, half):
-        one, two = ref[0:SPAN, :].astype(F32), ref[SPAN : 2 * SPAN, :].astype(F32)
-        return jnp.where(straight, (one, two)[half], (two, one)[half])
-
-    for half in range(2):
-        qb[0, half] = in_order(q_ref, half).astype(BF)
-        kvb[0, half, 0] = in_order(k_ref, half).astype(BF)
-        kvb[0, half, 1] = in_order(v_ref, half).astype(BF)
-    greet(
+    peers = (
         [{"seq": along_y[d]} for d in (1, 2, 3)]
         + [{"seq": along_z[d]} for d in (1, 3)]
         + [{"seq": (rank + d) % 16} for d in (1, 15)]
@@ -149,6 +141,33 @@
         + [{"mp": mp_of(zl, xs[d], 1 - core)} for d in (1, 2, 3)]
         + [{"mp": mp_of(lines[k], x)} for k in (1, 2, 3)]
     )
+    barrier = pltpu.get_barrier_semaphore()
+    for peer in peers:
+        pl.semaphore_signal(
+            barrier, inc=1, device_id=peer, device_id_type=pl.DeviceIdType.MESH
+        )
+    loads = [
+        pltpu.make_async_copy(src, dst, in_sem.at[k])
+        for k, (src, dst) in enumerate(zip(arrays, held))
+    ]
+    for load in loads:
+        load.start()
+    gap = slot_ref[2 * rank] - slot_ref[2 * rank + 1]
+    straight = jnp.full((SPAN, HD), gap, jnp.int32) < 0
+
+    def in_order(ref, half):
+        one, two = ref[0:SPAN, :].astype(F32), ref[SPAN : 2 * SPAN, :].astype(F32)
+        return jnp.where(straight, (one, two)[half], (two, one)[half])
+
+    for load in loads[:3]:
+        load.wait()
+    for half in range(2):
+        qb[0, half] = in_order(q_ref, half).astype(BF)
+        kvb[0, half, 0] = in_order(k_ref, half).astype(BF)
+        kvb[0, half, 1] = in_order(v_ref, half).astype(BF)
+    for load in loads[3:]:
+        load.wait()
+    pl.semaphore_wait(barrier, len(peers))
 
     def kv_copy(direction, half, sub, relay):
         source = 0 if not relay else (3 if direction == 0 else 1)
@@ -505,60 +524,62 @@
     low_relay(0)
     visit_all(0, 1, 1)
     kv_arrival(3, 0, 1).wait_recv()
-    send_high(0)
     visit_all(3, 0, 0)
     kv_arrival(1, 0, 0).wait_recv()
+    send_high(0)
+    visit_all(1, 0, 0)
     send_high(1)
-    visit_all(1, 0, 0)
     kv_arrival(2, 0, 0).wait_recv()
     kv_arrival(2, 0, 1).wait_recv()
-    visit_all(2, 0, 0)
+    visit_all(2, 0, 1)
     send_partial(0)
+    visit(0, 2, 0)
     low_relay(1)
     combine(0)
     own_out(0)
-    w_copy.wait_recv()
-    x_in(0, 0)
     kv_arrival(3, 1, 1).wait_recv()
     visit_all(3, 1, 0)
-    line_in(0, 1)
     kv_arrival(1, 1, 0).wait_recv()
     visit_all(1, 1, 0)
+    x_in(0, 0)
+    line_in(0, 1)
+    kv_arrival(2, 1, 0).wait_recv()
+    kv_arrival(2, 1, 1).wait_recv()
+    visit_all(2, 1, 1)
+    send_partial(1)
+    visit(0, 2, 1)
     line_in(0, 2)
     x_in(0, 1)
     line_in(0, 3)
-    kv_arrival(2, 1, 0).wait_recv()
-    kv_arrival(2, 1, 1).wait_recv()
-    visit_all(2, 1, 0)
-    send_partial(1)
+    w_copy.wait_recv()
+    combine(1)
+    own_out(1)
     project(0, 0)
     x_in(0, 2)
     project(0, 1)
-    combine(1)
-    own_out(1)
     x_in(0, 3)
-    project(0, 2)
     line_in(1, 1)
     x_in(1, 0)
     line_in(1, 2)
-    project(0, 3)
+    project(0, 2)
     line_in(1, 3)
     x_in(1, 1)
+    project(0, 3)
+    x_in(1, 2)
     finish(0)
     project(1, 0)
-    x_in(1, 2)
-    stat_late(0)
+    x_in(1, 3)
     project(1, 1)
-    x_in(1, 3)
-    normalize(0)
     project(1, 2)
     project(1, 3)
+    stat_late(0)
+    finish(1)
+    stat_late(1)
+    normalize(0)
     conv_own(0)
-    finish(1)
-    conv_rest(0)
-    stat_late(1)
     normalize(1)
     conv_own(1)
+    conv_rest(0)
     conv_rest(1)
     low, high = final[0], final[1]
     out_ref[0:SPAN, :] = jnp.where(straight, low, high).astype(BF)
@@ -609,9 +630,18 @@
     return pl.pallas_call(
         layer_kernel,
         out_shape=jax.ShapeDtypeStruct(queries.shape, BF),
-        in_specs=[pl.BlockSpec(memory_space=pltpu.SMEM)] + [vmem] * 9,
+        in_specs=[pl.BlockSpec(memory_space=pltpu.SMEM)] + [pl.BlockSpec(memory_space=pl.ANY)] * 9,
         out_specs=vmem,
         scratch_shapes=[
+            pltpu.VMEM((2 * SPAN, HD), BF),
+            pltpu.VMEM((2 * SPAN, HD), BF),
+            pltpu.VMEM((2 * SPAN, HD), BF),
+            pltpu.VMEM((16, 2, HD, HD), BF),
+            pltpu.VMEM((2 * SPAN, HD), BF),
+            pltpu.VMEM((HD, FILT), BF),
+            pltpu.VMEM((1, HD), F32),
+            pltpu.VMEM((1, HD), jnp.int32),
+            pltpu.VMEM((1, HD), F32),
             pltpu.VMEM((4, 2, SPAN, HD), BF),
             pltpu.VMEM((4, 2, 2, SPAN, HD), BF),
             pltpu.VMEM((4, 2, SPAN, HD), F32),
@@ -662,6 +692,7 @@
             dma((2,)),
             dma((2,)),
             dma((2,)),
+            dma((9,)),
         ],
         compiler_params=pltpu.CompilerParams(collective_id=0, has_side_effects=True),
         name="layer",
@@ -670,10 +701,10 @@
         queries,
         key_vecs,
         value_vecs,
+        w_out.reshape(16, 2, HD, HD),
         incoming,
-        w_out.reshape(16, 2, HD, HD),
+        filters,
         norm_gain.reshape(1, HD),
-        filters,
         filter_len.reshape(1, HD),
         skip_gain.reshape(1, HD),
     )

time: 105 us -> 96.6 us (0.920); the launches traced: 103 us -> 96.4 us
  Pallas kernels: 102 us -> 94.9 us
    pallas_call x1, Pallas kernels: 102 us -> 94.9 us  [on_device(): pl.pallas_call(layer_kernel, out_shape=jax.ShapeDtypeStruct(queries.shape...]
where the time goes in v4:
time: 96.6 us; the launch traced here: 96.4 us
  Pallas kernels  94.9 us (98%)
  local copies, waits for them, and re-layouts  1.57 us (2%)
    pallas_call x1, Pallas kernels, on_device(): pl.pallas_call(layer_kernel, out_shape=jax.ShapeDtypeStruct(queries.shape...  94.9 us

profile of v4, /device:TPU:1, one launch (start us, length us, event | category | flops | bytes accessed | tf_op | source)
XLA Modules:
  0.0 96.4 jit_solution(8489817434264893410)
XLA Ops:
  0.0 94.9 %layer.1 = bf16[512,128]{1,0:T(8,128)(2,1)} custom-call(s32[32]{0:T(128)} %slot_ref.1, bf16[512,128]{1,0:T(8,128)(2,1)} %q_hbm.1, bf16[512,128]{1,0:T(8,128)(2,1)} %k_hbm.1, bf16[512,128]{1,0:T(8,128)(2,1)} %v_hbm.1, bf16[16,2,128,128]{3,2,1,0:T(8,128)(2,1)} %bitcast.4, bf16[512,128]{1,0:T(8,128)(2,1)} %inc_hbm.1, bf16[128,256]{1,0:T(8,128)(2,1)} %filt_hbm.1, ...), custom_call_target="tpu_custom_call" | custom-call | tf_op jit(solution)/shard_map/layer/pallas_call | solution.py:630
  94.9 1.6 %copy.12 = bf16[512,128]{1,0:T(8,128)(2,1)} copy(bf16[512,128]{1,0:T(8,128)(2,1)} %layer.1) | data formatting | bytes 262144

commit v5 on v4

--- a/solution.py
+++ b/solution.py
@@ -81,8 +81,7 @@
     resid,
     taps,
     stat,
-    stat_x,
-    stat_z,
+    stat_all,
     rb,
     hb,
     scales,
@@ -106,10 +105,8 @@
     p_rsem,
     w_ssem,
     w_rsem,
-    tx_ssem,
-    tx_rsem,
-    tz_ssem,
-    tz_rsem,
+    t_ssem,
+    t_rsem,
     h_ssem,
     h_rsem,
     s_ssem,
@@ -136,16 +133,20 @@
         [{"seq": along_y[d]} for d in (1, 2, 3)]
         + [{"seq": along_z[d]} for d in (1, 3)]
         + [{"seq": (rank + d) % 16} for d in (1, 15)]
-        + [{"mp": partner}]
-        + [{"mp": mp_of(zl, xs[d])} for d in (1, 2, 3)]
-        + [{"mp": mp_of(zl, xs[d], 1 - core)} for d in (1, 2, 3)]
-        + [{"mp": mp_of(lines[k], x)} for k in (1, 2, 3)]
     )
     barrier = pltpu.get_barrier_semaphore()
     for peer in peers:
         pl.semaphore_signal(
             barrier, inc=1, device_id=peer, device_id_type=pl.DeviceIdType.MESH
         )
+
+    def greet(j, carry):
+        pl.semaphore_signal(
+            barrier, inc=1, device_id={"mp": (head + j) % 32}, device_id_type=pl.DeviceIdType.MESH
+        )
+        return carry
+
+    lax.fori_loop(1, 32, greet, 0)
     loads = [
         pltpu.make_async_copy(src, dst, in_sem.at[k])
         for k, (src, dst) in enumerate(zip(arrays, held))
@@ -167,7 +168,7 @@
         kvb[0, half, 1] = in_order(v_ref, half).astype(BF)
     for load in loads[3:]:
         load.wait()
-    pl.semaphore_wait(barrier, len(peers))
+    pl.semaphore_wait(barrier, len(peers) + 31)
 
     def kv_copy(direction, half, sub, relay):
         source = 0 if not relay else (3 if direction == 0 else 1)
@@ -238,41 +239,26 @@
             part_send.at[half], part_recv.at[half], p_ssem.at[half], p_rsem.at[half], mp=partner
         )
 
-    plane = [(d, c) for d in (2, 1, 3, 0) for c in (0, 1) if (d, c) != (0, 0)]
-
-    def sx_copy(half, d, flip):
+    def stat_copy(half, j):
         return remote(
-            stat.at[half, 0],
-            stat_x.at[half, x * 2 + core],
-            tx_ssem.at[half, d * 2 + flip],
-            tx_rsem.at[half, x * 2 + core],
-            mp=mp_of(zl, xs[d], core + flip - 2 * core * flip),
-        )
-
-    def sx_arrival(half, d, flip):
-        spot = xs[d] * 2 + core + flip - 2 * core * flip
-        view = stat_x.at[half, spot]
-        return remote(view, view, tx_ssem.at[half, 0], tx_rsem.at[half, spot], mp=head)
-
-    def sz_copy(half, k):
+            stat.at[half],
+            stat_all.at[half, head],
+            t_ssem.at[half],
+            t_rsem.at[half],
+            mp=(head + j) % 32,
+        )
+
+    def stat_others(half):
+        view = stat_all.at[half, pl.ds(0, 31)]
+        return remote(view, view, t_ssem.at[half], t_rsem.at[half], mp=head)
+
+    def h_copy(half, part):
+        rows = pl.ds(128 - 128 * part, 128)
         return remote(
-            stat.at[half, 1],
-            stat_z.at[half, zl],
-            tz_ssem.at[half, k],
-            tz_rsem.at[half, zl],
-            mp=mp_of(lines[k], x),
-        )
-
-    def sz_arrival(half, k):
-        view = stat_z.at[half, lines[k]]
-        return remote(view, view, tz_ssem.at[half, k], tz_rsem.at[half, lines[k]], mp=head)
-
-    def h_copy(half):
-        return remote(
-            rb.at[half],
-            hb.at[half],
-            h_ssem.at[half],
-            h_rsem.at[half],
+            rb.at[half, rows],
+            hb.at[half, rows],
+            h_ssem.at[half, part],
+            h_rsem.at[half, part],
             seq=(rank + (1 if half == 0 else 15)) % 16,
         )
 
@@ -417,35 +403,24 @@
         part_copy(half).wait_recv()
         whole = resid[half] + part_recv[half]
         square = whole * whole
-        stat[half, 0, 0:2] = jnp.concatenate(
-            [jnp.sum(square[k : k + 128].T, axis=0, keepdims=True) for k in (0, 128)], axis=0
-        )
-        for d, flip in plane:
-            sx_copy(half, d, flip).start()
         resid[half] = whole
         rb[half] = whole.astype(BF)
-
+        stat[half] = jnp.concatenate(
+            [jnp.sum(square[k : k + 128].T, axis=0, keepdims=True) for k in (0, 128)], axis=0
+        )
+        for j in range(31, 0, -1):
+            stat_copy(half, j).start()
+
+    def rows_out(half):
         @pl.when(rank != (15 if half == 0 else 0))
         def _():
-            h_copy(half).start()
-
-    def stat_late(half):
-        for d, flip in plane:
-            sx_arrival(half, d, flip).wait_recv()
-        stat_x[half, x * 2 + core, 0:2] = stat[half, 0, 0:2]
-        run = stat_x[half, 0, 0:2]
-        for k in range(1, 8):
-            run = run + stat_x[half, k, 0:2]
-        stat[half, 1, 0:2] = run
-        for k in (3, 2, 1):
-            sz_copy(half, k).start()
+            for part in range(2):
+                h_copy(half, part).start()
 
     def normalize(half):
-        for k in (1, 2, 3):
-            sz_arrival(half, k).wait_recv()
-        whole = stat[half, 1, 0:2]
-        for k in (1, 2, 3):
-            whole = whole + stat_z[half, lines[k], 0:2]
+        stat_others(half).wait_recv()
+        stat_all[half, head] = stat[half]
+        whole = jnp.sum(stat_all[half], axis=0)
         lane_scale = lax.rsqrt(whole / D + EPS)
         scales[half, 0:2] = lane_scale
 
@@ -484,20 +459,54 @@
             hb[half] = jnp.zeros((SPAN, HD), BF) if half == 0 else rb[0]
             hs[half, 0:2] = jnp.zeros((2, HD), F32) if half == 0 else scales[0, 0:2]
 
-        @pl.when(jnp.logical_not(edge))
-        def _():
-            h_copy(half).wait_recv()
-            s_copy(half).wait_recv()
-
-        rows = hb[half].astype(F32) * from_lanes(hs[half, 0:2]) * gain_ref[...]
-        before = rows.astype(BF).astype(F32)
-        for s in range(8):
-            shift[half, s, s : SPAN + s, :] = before
-        for top in range(0, SPAN, TILE):
-            begin = jnp.zeros((TILE, HD), F32) if top == 0 else conv[half, top : top + TILE, :]
-            final[half, top : top + TILE, :] = resid[half, top : top + TILE, :] + lags(
-                half, top, top // 8, FILT // 8, begin
-            )
+        def arrived(copy):
+            @pl.when(jnp.logical_not(edge))
+            def _():
+                copy.wait_recv()
+
+        arrived(s_copy(half))
+        for part in range(2):
+            at = 128 - 128 * part
+            arrived(h_copy(half, part))
+            scale = from_lanes(hs[half, 1 - part : 2 - part])
+            rows = hb[half, at : at + 128, :].astype(F32) * scale * gain_ref[...]
+            before = rows.astype(BF).astype(F32)
+            for s in range(8):
+                shift[half, s, at + s : at + s + 128, :] = before
+            for top in range(0, SPAN, TILE):
+                turn = min(FILT // 8, top // 8 + 15)
+                if part == 0:
+                    run = jnp.zeros((TILE, HD), F32) if top == 0 else conv[half, top : top + TILE, :]
+                    run = lags(half, top, top // 8, turn, run)
+                    if turn < FILT // 8:
+                        conv[half, top : top + TILE, :] = run
+                        continue
+                elif turn < FILT // 8:
+                    run = lags(half, top, turn, FILT // 8, conv[half, top : top + TILE, :])
+                else:
+                    continue
+                final[half, top : top + TILE, :] = resid[half, top : top + TILE, :] + run
+
+    def sent():
+        for half in range(2):
+            for direction in range(2):
+                for sub in range(2):
+                    kv_copy(direction, half, sub, False).wait_send()
+                kv_copy(direction, half, direction, True).wait_send()
+                for k in range(4):
+                    for sub in range(2):
+                        x_copy(half, k, direction, sub, False).wait_send()
+                    x_copy(half, k, direction, direction, True).wait_send()
+            part_copy(half).wait_send()
+            stat_others(half).wait_send()
+            for k in (1, 2, 3):
+                for copy in o_copies(k, half):
+                    copy.wait_send()
+                line_copy(half, k).wait_send()
+
+        w_copy.wait_send()
+        for d in (1, 2, 3):
+            q_copy(d).wait_send()
 
     def low_relay(half):
         kv_arrival(3, half, 0).wait_recv()
@@ -567,16 +576,17 @@
     project(0, 3)
     x_in(1, 2)
     finish(0)
+    rows_out(0)
     project(1, 0)
     x_in(1, 3)
     project(1, 1)
     project(1, 2)
     project(1, 3)
-    stat_late(0)
     finish(1)
-    stat_late(1)
     normalize(0)
     conv_own(0)
+    rows_out(1)
+    sent()
     normalize(1)
     conv_own(1)
     conv_rest(0)
@@ -586,31 +596,12 @@
     out_ref[SPAN : 2 * SPAN, :] = jnp.where(straight, high, low).astype(BF)
 
     for half in range(2):
-        for direction in range(2):
-            for sub in range(2):
-                kv_copy(direction, half, sub, False).wait_send()
-            kv_copy(direction, half, direction, True).wait_send()
-            for k in range(4):
-                for sub in range(2):
-                    x_copy(half, k, direction, sub, False).wait_send()
-                x_copy(half, k, direction, direction, True).wait_send()
-        part_copy(half).wait_send()
-        for d, flip in plane:
-            sx_copy(half, d, flip).wait_send()
-        for k in (1, 2, 3):
-            for copy in o_copies(k, half):
-                copy.wait_send()
-            line_copy(half, k).wait_send()
-            sz_copy(half, k).wait_send()
 
         @pl.when(rank != (15 if half == 0 else 0))
         def _():
-            h_copy(half).wait_send()
+            h_copy(half, 0).wait_send()
+            h_copy(half, 1).wait_send()
             s_copy(half).wait_send()
-
-    w_copy.wait_send()
-    for d in (1, 2, 3):
-        q_copy(d).wait_send()
 
 
 def on_device(
@@ -658,9 +649,8 @@
             pltpu.VMEM((2, SPAN, HD), F32),
             pltpu.VMEM((2, SPAN, HD), F32),
             pltpu.VMEM((FILT, HD), F32),
-            pltpu.VMEM((2, 2, 8, HD), F32),
-            pltpu.VMEM((2, 8, 8, HD), F32),
-            pltpu.VMEM((2, 4, 8, HD), F32),
+            pltpu.VMEM((2, 2, HD), F32),
+            pltpu.VMEM((2, 32, 2, HD), F32),
             pltpu.VMEM((2, SPAN, HD), BF),
             pltpu.VMEM((2, SPAN, HD), BF),
             pltpu.VMEM((2, 8, HD), F32),
@@ -684,12 +674,10 @@
             dma((2,)),
             dma((1,)),
             dma((1,)),
-            dma((2, 8)),
-            dma((2, 8)),
-            dma((2, 4)),
-            dma((2, 4)),
             dma((2,)),
             dma((2,)),
+            dma((2, 2)),
+            dma((2, 2)),
             dma((2,)),
             dma((2,)),
             dma((9,)),

time: 96.6 us -> 96.6 us (level)
  no operation moved by 1% of the time
where the time goes in v5:
time: 96.6 us; the launch traced here: 96.5 us
  Pallas kernels  94.9 us (98%)
  local copies, waits for them, and re-layouts  1.57 us (2%)
    pallas_call x1, Pallas kernels, on_device(): pl.pallas_call(layer_kernel, out_shape=jax.ShapeDtypeStruct(queries.shape...  94.9 us

profile of v5, /device:TPU:1, one launch (start us, length us, event | category | flops | bytes accessed | tf_op | source)
XLA Modules:
  0.0 96.5 jit_solution(13876665407377526173)
XLA Ops:
  0.0 94.9 %layer.1 = bf16[512,128]{1,0:T(8,128)(2,1)} custom-call(s32[32]{0:T(128)} %slot_ref.1, bf16[512,128]{1,0:T(8,128)(2,1)} %q_hbm.1, bf16[512,128]{1,0:T(8,128)(2,1)} %k_hbm.1, bf16[512,128]{1,0:T(8,128)(2,1)} %v_hbm.1, bf16[16,2,128,128]{3,2,1,0:T(8,128)(2,1)} %bitcast.4, bf16[512,128]{1,0:T(8,128)(2,1)} %inc_hbm.1, bf16[128,256]{1,0:T(8,128)(2,1)} %filt_hbm.1, ...), custom_call_target="tpu_custom_call" | custom-call | tf_op jit(solution)/shard_map/layer/pallas_call | solution.py:621
  94.9 1.6 %copy.12 = bf16[512,128]{1,0:T(8,128)(2,1)} copy(bf16[512,128]{1,0:T(8,128)(2,1)} %layer.1) | data formatting | bytes 262144

commit v6 on v5

--- a/solution.py
+++ b/solution.py
@@ -170,6 +170,9 @@
         load.wait()
     pl.semaphore_wait(barrier, len(peers) + 31)
 
+    def in_all(view, send_sem, recv_sem):
+        return remote(view, view, send_sem, recv_sem, mp=head)
+
     def kv_copy(direction, half, sub, relay):
         source = 0 if not relay else (3 if direction == 0 else 1)
         target = 2 if relay else (3 if direction == 0 else 1)
@@ -177,32 +180,32 @@
         return remote(
             kvb.at[source, half, :, rows],
             kvb.at[target, half, :, rows],
-            kv_ssem.at[direction, half, 2 if relay else sub],
-            kv_rsem.at[target, half, sub],
+            kv_ssem.at[0],
+            kv_rsem.at[target - 1, half, sub],
             seq=along_z[1 if direction == 0 else 3],
         )
 
     def kv_arrival(slot, half, sub):
         view = kvb.at[slot, half, :, pl.ds(sub * 128, 128)]
-        return remote(view, view, kv_ssem.at[0, half, sub], kv_rsem.at[slot, half, sub], seq=rank)
+        return remote(view, view, kv_ssem.at[0], kv_rsem.at[slot - 1, half, sub], seq=rank)
 
     def q_copy(d):
-        return remote(qb.at[0], qb.at[4 - d], q_ssem.at[d - 1], q_rsem.at[3 - d], seq=along_y[d])
+        return remote(qb.at[0], qb.at[4 - d], q_ssem.at[0], q_rsem.at[0], seq=along_y[d])
 
     def o_copies(d, half):
         return (
             remote(
                 osend.at[d - 1, half],
                 orecv.at[3 - d, half],
-                o_ssem.at[d - 1, half],
-                o_rsem.at[3 - d, half],
+                o_ssem.at[0],
+                o_rsem.at[half],
                 seq=along_y[d],
             ),
             remote(
                 lsend.at[d - 1, half],
                 lrecv.at[3 - d, half],
-                l_ssem.at[d - 1, half],
-                l_rsem.at[3 - d, half],
+                l_ssem.at[0],
+                l_rsem.at[half],
                 seq=along_y[d],
             ),
         )
@@ -210,12 +213,12 @@
     def line_copy(half, k):
         view = gath.at[half, zl, x]
         return remote(
-            view, view, z_ssem.at[half, k - 1], z_rsem.at[half, zl], mp=mp_of(lines[k], x)
+            view, view, z_ssem.at[0], z_rsem.at[half, zl], mp=mp_of(lines[k], x)
         )
 
     def line_arrival(half, k):
         view = gath.at[half, lines[k], x]
-        return remote(view, view, z_ssem.at[half, k - 1], z_rsem.at[half, lines[k]], mp=head)
+        return remote(view, view, z_ssem.at[0], z_rsem.at[half, lines[k]], mp=head)
 
     def x_copy(half, k, direction, sub, relay):
         source = xs[(3 if direction == 0 else 1) if relay else 0]
@@ -223,14 +226,14 @@
         return remote(
             view,
             view,
-            x_ssem.at[half, k, direction, 2 if relay else sub],
-            x_rsem.at[half, k, source, sub],
+            x_ssem.at[0],
+            x_rsem.at[half, k, 1 + direction if not relay and sub == direction else 0],
             mp=mp_of(zl, xs[1 if direction == 0 else 3]),
         )
 
     def x_arrival(half, k, d, sub):
         view = gath.at[half, lines[k], xs[d], pl.ds(sub * 128, 128)]
-        return remote(view, view, x_ssem.at[half, k, 0, sub], x_rsem.at[half, k, xs[d], sub], mp=head)
+        return remote(view, view, x_ssem.at[0], x_rsem.at[half, k, 1 + sub], mp=head)
 
     w_copy = remote(w_ref.at[:, 1 - core], w_pair, w_ssem.at[0], w_rsem.at[0], mp=partner)
 
@@ -340,9 +343,8 @@
                 copy.start()
 
     def combine(half):
-        for d in (1, 2, 3):
-            for copy in o_copies(d, half):
-                copy.wait_recv()
+        in_all(orecv.at[:, half], o_ssem.at[0], o_rsem.at[half]).wait_recv()
+        in_all(lrecv.at[:, half], l_ssem.at[0], l_rsem.at[half]).wait_recv()
         norm = jnp.maximum(total[0, half], 1e-30)
         logs = [peak[0, half] * LOG2 + jnp.log2(norm)]
         logs += [from_lanes(lrecv[s, half, 0:2]) for s in range(3)]
@@ -374,10 +376,7 @@
         x_copy(half, k, 1, 1, True).start()
 
     def project(half, k):
-        x_arrival(half, k, 3, 1).wait_recv()
-        x_arrival(half, k, 1, 0).wait_recv()
-        x_arrival(half, k, 2, 0).wait_recv()
-        x_arrival(half, k, 2, 1).wait_recv()
+        in_all(gath.at[half, 0, pl.ds(0, 2)], x_ssem.at[0], x_rsem.at[half, k, 0]).wait_recv()
         rows = jnp.concatenate([gath[half, lines[k], x_i] for x_i in range(4)], axis=1)
         weights = jnp.concatenate(
             [
@@ -488,25 +487,16 @@
                 final[half, top : top + TILE, :] = resid[half, top : top + TILE, :] + run
 
     def sent():
+        in_all(kvb.at[pl.ds(0, 3)], kv_ssem.at[0], kv_rsem.at[0, 0, 0]).wait_send()
+        in_all(qb.at[pl.ds(1, 3)], q_ssem.at[0], q_rsem.at[0]).wait_send()
+        in_all(osend, o_ssem.at[0], o_rsem.at[0]).wait_send()
+        in_all(lsend, l_ssem.at[0], l_rsem.at[0]).wait_send()
+        in_all(gath.at[:, pl.ds(0, 3), 0], z_ssem.at[0], z_rsem.at[0, 0]).wait_send()
+        in_all(gath.at[:, pl.ds(0, 3)], x_ssem.at[0], x_rsem.at[0, 0, 0]).wait_send()
         for half in range(2):
-            for direction in range(2):
-                for sub in range(2):
-                    kv_copy(direction, half, sub, False).wait_send()
-                kv_copy(direction, half, direction, True).wait_send()
-                for k in range(4):
-                    for sub in range(2):
-                        x_copy(half, k, direction, sub, False).wait_send()
-                    x_copy(half, k, direction, direction, True).wait_send()
             part_copy(half).wait_send()
             stat_others(half).wait_send()
-            for k in (1, 2, 3):
-                for copy in o_copies(k, half):
-                    copy.wait_send()
-                line_copy(half, k).wait_send()
-
         w_copy.wait_send()
-        for d in (1, 2, 3):
-            q_copy(d).wait_send()
 
     def low_relay(half):
         kv_arrival(3, half, 0).wait_recv()
@@ -527,8 +517,7 @@
         [filt_ref[:, k : k + 128].astype(F32).T for k in (0, 128)], axis=0
     )
     taps[...] = jnp.where(lag < flen_ref[...], turned, 0.0)
-    for d in (1, 2, 3):
-        q_copy(d).wait_recv()
+    in_all(qb.at[pl.ds(1, 3)], q_ssem.at[0], q_rsem.at[0]).wait_recv()
     visit_all(0, 0, 1)
     low_relay(0)
     visit_all(0, 1, 1)
@@ -658,18 +647,18 @@
             pltpu.VMEM((2, 8, 2 * SPAN + 8, HD), F32),
             pltpu.VMEM((2, SPAN, HD), F32),
             pltpu.VMEM((2, SPAN, HD), F32),
-            dma((3,)),
-            dma((3,)),
-            dma((2, 2, 3)),
-            dma((4, 2, 2)),
-            dma((3, 2)),
-            dma((3, 2)),
-            dma((3, 2)),
-            dma((3, 2)),
-            dma((2, 3)),
+            dma((1,)),
+            dma((1,)),
+            dma((1,)),
+            dma((3, 2, 2)),
+            dma((1,)),
+            dma((2,)),
+            dma((1,)),
+            dma((2,)),
+            dma((1,)),
             dma((2, 4)),
-            dma((2, 4, 2, 3)),
-            dma((2, 4, 4, 2)),
+            dma((1,)),
+            dma((2, 4, 3)),
             dma((2,)),
             dma((2,)),
             dma((1,)),

time: 96.6 us -> 95.1 us (0.984)
  Pallas kernels: 94.9 us -> 93.4 us
    pallas_call x1, Pallas kernels: 94.9 us -> 93.4 us  [on_device(): pl.pallas_call(layer_kernel, out_shape=jax.ShapeDtypeStruct(queries.shape...]
where the time goes in v6:
time: 95.1 us; the launch traced here: 94.9 us
  Pallas kernels  93.4 us (98%)
  local copies, waits for them, and re-layouts  1.57 us (2%)
    pallas_call x1, Pallas kernels, on_device(): pl.pallas_call(layer_kernel, out_shape=jax.ShapeDtypeStruct(queries.shape...  93.4 us

profile of v6, /device:TPU:1, one launch (start us, length us, event | category | flops | bytes accessed | tf_op | source)
XLA Modules:
  0.0 94.9 jit_solution(4279269980770062717)
XLA Ops:
  0.0 93.4 %layer.1 = bf16[512,128]{1,0:T(8,128)(2,1)} custom-call(s32[32]{0:T(128)} %slot_ref.1, bf16[512,128]{1,0:T(8,128)(2,1)} %q_hbm.1, bf16[512,128]{1,0:T(8,128)(2,1)} %k_hbm.1, bf16[512,128]{1,0:T(8,128)(2,1)} %v_hbm.1, bf16[16,2,128,128]{3,2,1,0:T(8,128)(2,1)} %bitcast.4, bf16[512,128]{1,0:T(8,128)(2,1)} %inc_hbm.1, bf16[128,256]{1,0:T(8,128)(2,1)} %filt_hbm.1, ...), custom_call_target="tpu_custom_call" | custom-call | tf_op jit(solution)/shard_map/layer/pallas_call | solution.py:610
  93.4 1.6 %copy.12 = bf16[512,128]{1,0:T(8,128)(2,1)} copy(bf16[512,128]{1,0:T(8,128)(2,1)} %layer.1) | data formatting | bytes 262144

commit v7 on v6

--- a/solution.py
+++ b/solution.py
@@ -44,7 +44,7 @@
 
 
 def layer_kernel(
-    slot_ref,
+    slot_hbm,
     q_hbm,
     k_hbm,
     v_hbm,
@@ -55,6 +55,7 @@
     flen_hbm,
     skip_hbm,
     out_ref,
+    slot_ref,
     q_ref,
     k_ref,
     v_ref,
@@ -113,8 +114,12 @@
     s_rsem,
     in_sem,
 ):
-    arrays = (q_hbm, k_hbm, v_hbm, w_hbm, inc_hbm, filt_hbm, gain_hbm, flen_hbm, skip_hbm)
-    held = (q_ref, k_ref, v_ref, w_ref, inc_ref, filt_ref, gain_ref, flen_ref, skip_ref)
+    arrays = (
+        slot_hbm, q_hbm, k_hbm, v_hbm, w_hbm, inc_hbm, filt_hbm, gain_hbm, flen_hbm, skip_hbm
+    )
+    held = (
+        slot_ref, q_ref, k_ref, v_ref, w_ref, inc_ref, filt_ref, gain_ref, flen_ref, skip_ref
+    )
     rank, head = lax.axis_index("seq"), lax.axis_index("mp")
     y, zh = rank // 4, rank % 4
     along_y = [((y + d) % 4) * 4 + zh for d in range(4)]
@@ -153,6 +158,7 @@
     ]
     for load in loads:
         load.start()
+    loads[0].wait()
     gap = slot_ref[2 * rank] - slot_ref[2 * rank + 1]
     straight = jnp.full((SPAN, HD), gap, jnp.int32) < 0
 
@@ -160,13 +166,13 @@
         one, two = ref[0:SPAN, :].astype(F32), ref[SPAN : 2 * SPAN, :].astype(F32)
         return jnp.where(straight, (one, two)[half], (two, one)[half])
 
-    for load in loads[:3]:
+    for load in loads[1:4]:
         load.wait()
     for half in range(2):
         qb[0, half] = in_order(q_ref, half).astype(BF)
         kvb[0, half, 0] = in_order(k_ref, half).astype(BF)
         kvb[0, half, 1] = in_order(v_ref, half).astype(BF)
-    for load in loads[3:]:
+    for load in loads[4:]:
         load.wait()
     pl.semaphore_wait(barrier, len(peers) + 31)
 
@@ -285,16 +291,21 @@
     peak[...] = jnp.full_like(peak, NEG)
     ones = jnp.ones((SPAN, HD), BF)
 
-    def block(d, qhalf, slot, half, diagonal):
+    def block(d, qhalf, slot, half, diagonal, count=1):
+        rows = count * SPAN
+        some = pl.ds(d, count)
         keys, values = kvb[slot, half, 0], kvb[slot, half, 1]
         scores = lax.dot_general(
-            qb[d, qhalf], keys, (((1,), (1,)), ((), ())), preferred_element_type=F32
+            qb[some, qhalf].reshape(rows, HD),
+            keys,
+            (((1,), (1,)), ((), ())),
+            preferred_element_type=F32,
         )
         if diagonal:
             row = lax.broadcasted_iota(jnp.int32, (SPAN, SPAN), 0)
             col = lax.broadcasted_iota(jnp.int32, (SPAN, SPAN), 1)
             scores = jnp.where(col <= row, scores, NEG)
-        old = peak[d, qhalf]
+        old = peak[some, qhalf].reshape(rows, HD)
         new = jnp.maximum(old, jnp.max(scores, axis=1, keepdims=True))
         weights = jnp.exp2((scores - jnp.concatenate([new, new], axis=1)) * LOG2)
         factor = jnp.exp2((old - new) * LOG2)
@@ -304,15 +315,17 @@
             (((1,), (0,)), ((), ())),
             preferred_element_type=F32,
         )
-        acc[d, qhalf] = acc[d, qhalf] * factor + summed[:, :HD]
-        total[d, qhalf] = total[d, qhalf] * factor + summed[:, HD:]
-        peak[d, qhalf] = new
+        shape = (count, SPAN, HD)
+        acc[some, qhalf] = (acc[some, qhalf].reshape(rows, HD) * factor + summed[:, :HD]).reshape(shape)
+        total[some, qhalf] = (
+            total[some, qhalf].reshape(rows, HD) * factor + summed[:, HD:]
+        ).reshape(shape)
+        peak[some, qhalf] = new.reshape(shape)
 
     def visit(d, slot, half):
         q_low = ((y + d) % 4) * 4 + zh
         k_low = y * 4 + (zh + slot) % 4
         if half == 0:
-            block(d, 1, slot, 0, False)
 
             @pl.when(k_low < q_low)
             def _():
@@ -328,7 +341,18 @@
             visit(d, slot, half)
             return carry
 
-        lax.fori_loop(start, 4, step, 0)
+        if half == 0:
+            if start == 0:
+                block(0, 1, slot, 0, False)
+            block(1, 1, slot, 0, False)
+            block(2, 1, slot, 0, False, 2)
+            lax.fori_loop(start, 4, step, 0)
+        else:
+            @pl.when(y >= 2)
+            def _():
+                block(2, 1, slot, 1, False, 2)
+
+            lax.fori_loop(start, jnp.where(y >= 2, 2, 4), step, 0)
 
     def send_partial(half):
         def step(d, carry):
@@ -531,6 +555,7 @@
     kv_arrival(2, 0, 1).wait_recv()
     visit_all(2, 0, 1)
     send_partial(0)
+    block(0, 1, 2, 0, False)
     visit(0, 2, 0)
     low_relay(1)
     combine(0)
@@ -610,9 +635,10 @@
     return pl.pallas_call(
         layer_kernel,
         out_shape=jax.ShapeDtypeStruct(queries.shape, BF),
-        in_specs=[pl.BlockSpec(memory_space=pltpu.SMEM)] + [pl.BlockSpec(memory_space=pl.ANY)] * 9,
+        in_specs=[pl.BlockSpec(memory_space=pl.ANY)] * 10,
         out_specs=vmem,
         scratch_shapes=[
+            pltpu.SMEM((32,), jnp.int32),
             pltpu.VMEM((2 * SPAN, HD), BF),
             pltpu.VMEM((2 * SPAN, HD), BF),
             pltpu.VMEM((2 * SPAN, HD), BF),
@@ -669,7 +695,7 @@
             dma((2, 2)),
             dma((2,)),
             dma((2,)),
-            dma((9,)),
+            dma((10,)),
         ],
         compiler_params=pltpu.CompilerParams(collective_id=0, has_side_effects=True),
         name="layer",

time: 95.1 us -> 92.6 us (0.974)
  Pallas kernels: 93.4 us -> 90.8 us
    pallas_call x1, Pallas kernels: 93.4 us -> 90.8 us  [on_device(): pl.pallas_call(layer_kernel, out_shape=jax.ShapeDtypeStruct(queries.shape...]
where the time goes in v7:
time: 92.6 us; the launch traced here: 92.4 us
  Pallas kernels  90.8 us (98%)
  local copies, waits for them, and re-layouts  1.57 us (2%)
    pallas_call x1, Pallas kernels, on_device(): pl.pallas_call(layer_kernel, out_shape=jax.ShapeDtypeStruct(queries.shape...  90.8 us

profile of v7, /device:TPU:1, one launch (start us, length us, event | category | flops | bytes accessed | tf_op | source)
XLA Modules:
  0.0 92.4 jit_solution(13076981819290375575)
XLA Ops:
  0.0 90.8 %layer.1 = bf16[512,128]{1,0:T(8,128)(2,1)} custom-call(s32[32]{0:T(128)} %slot_hbm.1, bf16[512,128]{1,0:T(8,128)(2,1)} %q_hbm.1, bf16[512,128]{1,0:T(8,128)(2,1)} %k_hbm.1, bf16[512,128]{1,0:T(8,128)(2,1)} %v_hbm.1, bf16[16,2,128,128]{3,2,1,0:T(8,128)(2,1)} %bitcast.4, bf16[512,128]{1,0:T(8,128)(2,1)} %inc_hbm.1, bf16[128,256]{1,0:T(8,128)(2,1)} %filt_hbm.1, ...), custom_call_target="tpu_custom_call" | custom-call | tf_op jit(solution)/shard_map/layer/pallas_call | solution.py:635
  90.8 1.6 %copy.12 = bf16[512,128]{1,0:T(8,128)(2,1)} copy(bf16[512,128]{1,0:T(8,128)(2,1)} %layer.1) | data formatting | bytes 262144

commit v8 on v7

--- a/solution.py
+++ b/solution.py
@@ -606,8 +606,8 @@
     conv_rest(0)
     conv_rest(1)
     low, high = final[0], final[1]
-    out_ref[0:SPAN, :] = jnp.where(straight, low, high).astype(BF)
-    out_ref[SPAN : 2 * SPAN, :] = jnp.where(straight, high, low).astype(BF)
+    out_ref[0:SPAN, :] = jnp.where(straight, low, high)
+    out_ref[SPAN : 2 * SPAN, :] = jnp.where(straight, high, low)
 
     for half in range(2):
 
@@ -634,7 +634,7 @@
     vmem = pl.BlockSpec(memory_space=pltpu.VMEM)
     return pl.pallas_call(
         layer_kernel,
-        out_shape=jax.ShapeDtypeStruct(queries.shape, BF),
+        out_shape=pltpu.VMEM(queries.shape, F32),
         in_specs=[pl.BlockSpec(memory_space=pl.ANY)] * 10,
         out_specs=vmem,
         scratch_shapes=[
@@ -710,7 +710,7 @@
         norm_gain.reshape(1, HD),
         filter_len.reshape(1, HD),
         skip_gain.reshape(1, HD),
-    )
+    ).astype(BF)
 
 
 def solution(mesh):

time: 92.6 us -> 91 us (0.983)
  local copies, waits for them, and re-layouts: 1.57 us -> 0 us
    unnamed x1 -> x0, local copies, waits for them, and re-layouts: 1.57 us -> none
where the time goes in v8:
time: 91 us; the launch traced here: 90.9 us
  Pallas kernels  90.2 us (99%)
    pallas_call x1, Pallas kernels, on_device(): pl.pallas_call(layer_kernel, out_shape=pltpu.VMEM(queries.shape, F32), in...  90.2 us

profile of v8, /device:TPU:1, one launch (start us, length us, event | category | flops | bytes accessed | tf_op | source)
XLA Modules:
  0.0 90.9 jit_solution(16773007309321968783)
XLA Ops:
  0.0 90.2 %layer.1 = f32[512,128]{1,0:T(8,128)S(1)} custom-call(s32[32]{0:T(128)} %slot_hbm.1, bf16[512,128]{1,0:T(8,128)(2,1)} %q_hbm.1, bf16[512,128]{1,0:T(8,128)(2,1)} %k_hbm.1, bf16[512,128]{1,0:T(8,128)(2,1)} %v_hbm.1, bf16[16,2,128,128]{3,2,1,0:T(8,128)(2,1)} %bitcast.4, bf16[512,128]{1,0:T(8,128)(2,1)} %inc_hbm.1, bf16[128,256]{1,0:T(8,128)(2,1)} %filt_hbm.1, ...), custom_call_target="tpu_custom_call" | custom-call | tf_op jit(solution)/shard_map/layer/pallas_call | solution.py:635
  90.2 0.7 convert_element_type.3

commit v9 on v8

--- a/solution.py
+++ b/solution.py
@@ -355,13 +355,10 @@
             lax.fori_loop(start, jnp.where(y >= 2, 2, 4), step, 0)
 
     def send_partial(half):
-        def step(d, carry):
+        for d in (2, 1, 3):
             norm = jnp.maximum(total[d, half], 1e-30)
             osend[d - 1, half] = (acc[d, half] / norm).astype(BF)
             lsend[d - 1, half, 0:2] = to_lanes(peak[d, half] * LOG2 + jnp.log2(norm))
-            return carry
-
-        lax.fori_loop(1, 4, step, 0)
         for d in (2, 1, 3):
             for copy in o_copies(d, half):
                 copy.start()

time: 91 us -> 90.9 us (level)
  no operation moved by 1% of the time
where the time goes in v9:
time: 90.9 us; the launch traced here: 90.8 us
  Pallas kernels  90.1 us (99%)
    pallas_call x1, Pallas kernels, on_device(): pl.pallas_call(layer_kernel, out_shape=pltpu.VMEM(queries.shape, F32), in...  90.1 us

profile of v9, /device:TPU:1, one launch (start us, length us, event | category | flops | bytes accessed | tf_op | source)
XLA Modules:
  0.0 90.8 jit_solution(7927693474500288378)
XLA Ops:
  0.0 90.1 %layer.1 = f32[512,128]{1,0:T(8,128)S(1)} custom-call(s32[32]{0:T(128)} %slot_hbm.1, bf16[512,128]{1,0:T(8,128)(2,1)} %q_hbm.1, bf16[512,128]{1,0:T(8,128)(2,1)} %k_hbm.1, bf16[512,128]{1,0:T(8,128)(2,1)} %v_hbm.1, bf16[16,2,128,128]{3,2,1,0:T(8,128)(2,1)} %bitcast.4, bf16[512,128]{1,0:T(8,128)(2,1)} %inc_hbm.1, bf16[128,256]{1,0:T(8,128)(2,1)} %filt_hbm.1, ...), custom_call_target="tpu_custom_call" | custom-call | tf_op jit(solution)/shard_map/layer/pallas_call | solution.py:632
  90.1 0.7 convert_element_type.3
